TPU v7x, 8 devices: a whole 2x2x1 slice. The times are simulated.
8 devices in a mesh: col: 4 (over z, y, x), row: 2 (over core).
Axes of the slice: x: 2, y: 2, z: 1, core: 2. Of those that a mesh axis runs over, the one named last changes fastest.
Arguments:
- vel_u: float32 [30, 128, 2048], P(None, 'row', 'col')
- vel_v: float32 [30, 128, 2048], P(None, 'row', 'col')
- temperature: float32 [30, 128, 2048], P(None, 'row', 'col')
- salinity: float32 [30, 128, 2048], P(None, 'row', 'col')
- surf_eta: float32 [128, 2048], P('row', 'col')
- trans_u: float32 [128, 2048], P('row', 'col')
- trans_v: float32 [128, 2048], P('row', 'col')
- bottom_depth: float32 [128, 2048], P('row', 'col')
- level_count: int32 [128, 2048], P('row', 'col')
- avg_weights: float32 [30], replicated
Outputs:
- output 1: float32 [128, 2048], P('row', 'col')
- output 2: float32 [128, 2048], P('row', 'col')
- output 3: float32 [128, 2048], P('row', 'col')
- output 4: float32 [30, 128, 2048], P(None, 'row', 'col')
- output 5: float32 [30, 128, 2048], P(None, 'row', 'col')
- output 6: float32 [30, 128, 2048], P(None, 'row', 'col')
- output 7: float32 [30, 128, 2048], P(None, 'row', 'col')
All inputs are finite; a program needn't handle non-finite values.
Results may differ from a plain program's by a relative error of at most 0.001.
Values sent between devices are 32-bit elements.
A program may use at most 1 GiB of HBM per device.

v0:
```python
import jax
import jax.numpy as jnp
from jax import lax
from jax.sharding import PartitionSpec as P

TIME_STEP = 1.0
GRAVITY = 16.0
BC_GRAVITY = 4.0
EXPAND_T = 0.2
CONTRACT_S = 0.6
CORIO_F0 = 0.4
CORIO_BETA = 0.4
VISC_R = 2.0
DIFF_R = 0.5


def shifted(padded, step_y, step_x):
    n_rows = padded.shape[-2] - 2
    n_cols = padded.shape[-1] - 2
    return padded[..., 1 + step_y:1 + step_y + n_rows, 1 + step_x:1 + step_x + n_cols]


def tri_solve(right_side, active, strength):
    link = strength * active[1:]
    zero_row = jnp.zeros_like(right_side[:1])
    low_links = jnp.concatenate([zero_row, link], axis=0)
    up_links = jnp.concatenate([link, zero_row], axis=0)

    def down(carry, level):
        ratio_prev, value_prev = carry
        low_link, up_link, target = level
        denominator = 1.0 + low_link + up_link + low_link * ratio_prev
        ratio = -up_link / denominator
        value = (target + low_link * value_prev) / denominator
        return (ratio, value), (ratio, value)

    start = (jnp.zeros_like(right_side[0]), jnp.zeros_like(right_side[0]))
    _, (ratios, values) = lax.scan(down, start, (low_links, up_links, right_side))

    def back(below, level):
        ratio, value = level
        solved = value - ratio * below
        return solved, solved

    _, solved_all = lax.scan(back, jnp.zeros_like(right_side[0]), (ratios, values), reverse=True)
    return solved_all


def ocean_columns(u_pad, v_pad, array_b15, salinity_pad, count_pad, depth_pad, coriolis_u, coriolis_v):
    n_levels = u_pad.shape[0]
    count_mid = shifted(count_pad, 0, 0)
    levels_u = jnp.minimum(count_mid, shifted(count_pad, 0, 1))
    levels_uw = jnp.minimum(shifted(count_pad, 0, -1), count_mid)
    levels_v = jnp.minimum(count_mid, shifted(count_pad, 1, 0))
    levels_vs = jnp.minimum(shifted(count_pad, -1, 0), count_mid)
    level_index = jnp.arange(n_levels)[:, None, None]
    mask_mid = (level_index < count_mid).astype(jnp.float32)
    mask_u = (level_index < levels_u).astype(jnp.float32)
    mask_uw = (level_index < levels_uw).astype(jnp.float32)
    mask_v = (level_index < levels_v).astype(jnp.float32)
    mask_vs = (level_index < levels_vs).astype(jnp.float32)
    u_mid = shifted(u_pad, 0, 0)
    v_mid = shifted(v_pad, 0, 0)
    u_west = shifted(u_pad, 0, -1)
    v_south = shifted(v_pad, -1, 0)
    v_at_u = 0.25 * (v_mid + shifted(v_pad, 0, 1) + v_south + shifted(v_pad, -1, 1))
    u_at_v = 0.25 * (u_mid + u_west + shifted(u_pad, 1, 0) + shifted(u_pad, 1, -1))
    inertia_u = 0.5 * (u_mid * (shifted(u_pad, 0, 1) - u_west) + v_at_u * (shifted(u_pad, 1, 0) - shifted(u_pad, -1, 0)))
    inertia_v = 0.5 * (u_at_v * (shifted(v_pad, 0, 1) - shifted(v_pad, 0, -1)) + v_mid * (shifted(v_pad, 1, 0) - v_south))
    density = CONTRACT_S * salinity_pad - EXPAND_T * array_b15
    pressure = (BC_GRAVITY / n_levels) * (jnp.cumsum(density, axis=0) - 0.5 * density)
    pressure_mid = shifted(pressure, 0, 0)
    u_star = u_mid + TIME_STEP * (coriolis_u * v_at_u - inertia_u - shifted(pressure, 0, 1) + pressure_mid)
    v_star = v_mid + TIME_STEP * (-coriolis_v * u_at_v - inertia_v - shifted(pressure, 1, 0) + pressure_mid)
    u_visc = tri_solve(u_star, mask_u, VISC_R)
    v_visc = tri_solve(v_star, mask_v, VISC_R)
    count_u = jnp.maximum(jnp.sum(mask_u, axis=0), 1.0)
    count_v = jnp.maximum(jnp.sum(mask_v, axis=0), 1.0)
    depth_mid = shifted(depth_pad, 0, 0)
    depth_u = 0.5 * (depth_mid + shifted(depth_pad, 0, 1))
    depth_v = 0.5 * (depth_mid + shifted(depth_pad, 1, 0))
    force_u = depth_u * jnp.sum(mask_u * (u_visc - u_mid), axis=0) / count_u / TIME_STEP
    force_v = depth_v * jnp.sum(mask_v * (v_visc - v_mid), axis=0) / count_v / TIME_STEP
    shear_u = u_visc - jnp.sum(mask_u * u_visc, axis=0) / count_u
    shear_v = v_visc - jnp.sum(mask_v * v_visc, axis=0) / count_v
    wet_u = (levels_u > 0).astype(jnp.float32)
    wet_v = (levels_v > 0).astype(jnp.float32)

    def advect(tracer_pad):
        tracer_mid = shifted(tracer_pad, 0, 0)
        flux_east = mask_u * u_mid * (tracer_mid + shifted(tracer_pad, 0, 1))
        flux_west = mask_uw * u_west * (shifted(tracer_pad, 0, -1) + tracer_mid)
        flux_north = mask_v * v_mid * (tracer_mid + shifted(tracer_pad, 1, 0))
        flux_south = mask_vs * v_south * (shifted(tracer_pad, -1, 0) + tracer_mid)
        return tracer_mid - 0.5 * TIME_STEP * (flux_east - flux_west + flux_north - flux_south)

    value_a15 = tri_solve(advect(array_b15), mask_mid, DIFF_R)
    salinity_new = tri_solve(advect(salinity_pad), mask_mid, DIFF_R)
    return (shear_u, shear_v, mask_u, mask_v, depth_u, depth_v, wet_u, wet_v, force_u, force_v, value_a15, salinity_new)


def fast_update(stack_pad, force_u, force_v, depth_u, depth_v, wet_u, wet_v, coriolis_u, coriolis_v, dt_fast):
    eta_pad = stack_pad[0]
    trans_u_pad = stack_pad[1]
    trans_v_pad = stack_pad[2]
    eta_ext = eta_pad[1:, 1:] - dt_fast * (trans_u_pad[1:, 1:] - trans_u_pad[1:, :-1] + trans_v_pad[1:, 1:] - trans_v_pad[:-1, 1:])
    eta_new = eta_ext[:-1, :-1]
    trans_u_old = shifted(trans_u_pad, 0, 0)
    trans_v_old = shifted(trans_v_pad, 0, 0)
    v_at_u = 0.25 * (trans_v_old + shifted(trans_v_pad, 0, 1) + shifted(trans_v_pad, -1, 0) + shifted(trans_v_pad, -1, 1))
    u_at_v = 0.25 * (trans_u_old + shifted(trans_u_pad, 0, -1) + shifted(trans_u_pad, 1, 0) + shifted(trans_u_pad, 1, -1))
    trans_u_new = wet_u * (trans_u_old + dt_fast * (coriolis_u * v_at_u + force_u - GRAVITY * depth_u * (eta_ext[:-1, 1:] - eta_new)))
    trans_v_new = wet_v * (trans_v_old + dt_fast * (force_v - coriolis_v * u_at_v - GRAVITY * depth_v * (eta_ext[1:, :-1] - eta_new)))
    return eta_new, trans_u_new, trans_v_new


def solution(mesh):
    n_col = mesh.shape['col']
    n_row = mesh.shape['row']
    east_moves = [(index, (index + 1) % n_col) for index in range(n_col)]
    west_moves = [(index, (index - 1) % n_col) for index in range(n_col)]
    north_moves = [(index, index + 1) for index in range(n_row - 1)]
    south_moves = [(index + 1, index) for index in range(n_row - 1)]

    def exchange(field):
        from_west = lax.ppermute(field[..., -1:], 'col', east_moves)
        from_east = lax.ppermute(field[..., :1], 'col', west_moves)
        wide = jnp.concatenate([from_west, field, from_east], axis=-1)
        from_south = lax.ppermute(wide[..., -1:, :], 'row', north_moves)
        from_north = lax.ppermute(wide[..., :1, :], 'row', south_moves)
        return jnp.concatenate([from_south, wide, from_north], axis=-2)

    def step(vel_u, vel_v, value_a11, salinity, surf_eta, trans_u, trans_v, bottom_depth, level_count, avg_weights):
        n_rows = surf_eta.shape[0]
        total_rows = n_rows * n_row
        dt_fast = TIME_STEP / avg_weights.shape[0]
        row_pos = (lax.axis_index('row') * n_rows + jnp.arange(n_rows)).astype(jnp.float32)[:, None]
        coriolis_u = CORIO_F0 + CORIO_BETA * ((row_pos + 0.5) / total_rows - 0.5)
        coriolis_v = CORIO_F0 + CORIO_BETA * ((row_pos + 1.0) / total_rows - 0.5)
        columns = ocean_columns(exchange(vel_u), exchange(vel_v), exchange(value_a11), exchange(salinity), exchange(level_count), exchange(bottom_depth), coriolis_u, coriolis_v)
        shear_u, shear_v, mask_u, mask_v, depth_u, depth_v, wet_u, wet_v, force_u, force_v, value_a15, salinity_new = columns

        def subcycle(carry, weight):
            eta_old, trans_u_old, trans_v_old, acc_u, acc_v = carry
            stack_pad = exchange(jnp.stack([eta_old, trans_u_old, trans_v_old]))
            eta_new, trans_u_new, trans_v_new = fast_update(stack_pad, force_u, force_v, depth_u, depth_v, wet_u, wet_v, coriolis_u, coriolis_v, dt_fast)
            return (eta_new, trans_u_new, trans_v_new, acc_u + weight * trans_u_new, acc_v + weight * trans_v_new), None

        zero_field = jnp.zeros_like(surf_eta)
        final, _ = lax.scan(subcycle, (surf_eta, trans_u, trans_v, zero_field, zero_field), avg_weights)
        eta_fin, trans_u_fin, trans_v_fin, bar_u, bar_v = final
        vel_u_new = mask_u * (shear_u + bar_u / depth_u)
        vel_v_new = mask_v * (shear_v + bar_v / depth_v)
        return (eta_fin, trans_u_fin, trans_v_fin, vel_u_new, vel_v_new, value_a15, salinity_new)

    cube = P(None, 'row', 'col')
    flat = P('row', 'col')
    return jax.shard_map(step, mesh=mesh, in_specs=(cube, cube, cube, cube, flat, flat, flat, flat, flat, P()), out_specs=(flat, flat, flat, cube, cube, cube, cube), check_vma=False)
```

profile of v0, /device:TPU:0, one launch (start us, length us, event | category | flops | bytes accessed | tf_op | source)
XLA Modules:
  0.0 1185.7 jit_solution(10613878078199087342)
XLA Ops:
  21.1 8.2 fusion.130
  45.6 4.3 fusion.132
  50.9 4.4 fusion.131
  74.8 3.7 collective-permute-start.8
  89.9 4.2 collective-permute-start.19
  100.1 9.9 fusion.47
  114.9 55.7 %while.163 = (s32[]{:T(128)}, f32[64,512]{1,0:T(8,128)S(1)}, f32[64,512]{1,0:T(8,128)S(1)}, f32[30,64,512]{2,1,0:T(8,128)}, f32[30,64,512]{2,1,0:T(8,128)}, /*in...) while((s32[]{:T(128)}, f32[64,512]{1,0:T(8,128)S(1)}, ...), condition=%wide.region_22.23_spmd.clone, body=%wide.region_21.22_spmd.clone.sunk | while | flops 360451 | bytes 1180271 | solution.py:38
  173.0 51.9 %while.164 = (s32[]{:T(128)}, f32[64,512]{1,0:T(8,128)S(1)}, f32[30,64,512]{2,1,0:T(8,128)}, f32[30,64,512]{2,1,0:T(8,128)}, f32[30,64,512]{2,1,0:T(8,128)}, /*index=5*/s32[]{:T(128)}, s32[]{:T(128)}, s32[]{:T(128)}) while((s32[]{:T(128)}, f32[64,512]{1,0:T(8,128)S(1)}, f32[30,64,512]{2,1,0:T(8,128)}, ...), condition=%wide.region_24.25_spmd.clone, body=%wide.region_23.24_spmd.clone.sunk | while | flops 98308 | bytes 655471 | solution.py:45
  224.9 4.8 collective-permute-start.12
  231.1 19.7 %fusion.60 = f32[30,64,512]{2,1,0:T(8,128)} fusion(f32[30,64,512]{2,1,0:T(8,128)} %param.30, f32[30,1,514]{2,1,0:T(1,128)} %collective-permute-done.19, f32[30,64,1]{2,1,0:T(8,128)} %copy-done.17, f32[30,64,1]{2,1,0:T(8,128)} %copy.34, f32[30,1,514]{2,1,0:T(1,128)} %collective-permute-done.20, f32[30,64,512]{2,1,0:T(8,128)} %param.28, ...), kind=kLoop, calls=%fused_computation.136 | loop fusion | flops 29491200 | bytes 20331488 | tf_op jit(solution)/shard_map/sub | solution.py:95
  255.6 55.7 %while.161 = (s32[]{:T(128)}, f32[64,512]{1,0:T(8,128)S(1)}, f32[64,512]{1,0:T(8,128)S(1)}, f32[30,64,512]{2,1,0:T(8,128)}, f32[30,64,512]{2,1,0:T(8,128)}, /*in...) while((s32[]{:T(128)}, f32[64,512]{1,0:T(8,128)S(1)}, ...), condition=%wide.region_18.19_spmd.clone, body=%wide.region_17.18_spmd.clone.sunk | while | flops 360451 | bytes 1180271 | solution.py:38
  313.7 51.9 %while.162 = (s32[]{:T(128)}, f32[64,512]{1,0:T(8,128)S(1)}, f32[30,64,512]{2,1,0:T(8,128)}, f32[30,64,512]{2,1,0:T(8,128)}, f32[30,64,512]{2,1,0:T(8,128)}, /*index=5*/s32[]{:T(128)}, s32[]{:T(128)}, s32[]{:T(128)}) while((s32[]{:T(128)}, f32[64,512]{1,0:T(8,128)S(1)}, f32[30,64,512]{2,1,0:T(8,128)}, ...), condition=%wide.region_20.21_spmd.clone, body=%wide.region_19.20_spmd.clone.sunk | while | flops 98308 | bytes 655471 | solution.py:45
  365.6 65.6 %subtract_multiply_fusion = f32[30,66,514]{2,1,0:T(8,128)} fusion(f32[30,1,514]{2,1,0:T(1,128)} %collective-permute-done.20, f32[30,64,1]{2,1,0:T(8,128)} %copy-done.17, f32[30,64,512]{2,1,0:T(8,128)} %param.30, f32[30,64,1]{2,1,0:T(8,128)} %copy.34, f32[30,1,514]{2,1,0:T(1,128)} %collective-permute-done.19, f32[30,1,514]{2,1,0:T(1,128)S(1)} %copy-done.37, ...), kind=kOutput, calls=%fused_computation.109 | output fusion | flops 54956880 | bytes 12212640 | tf_op jit(solution)/shard_map/jit(cumsum)/reduce_window_sum | solution.py:71
  431.2 4.2 pad_maximum_fusion.9
  436.0 16.9 %fusion.79 = f32[30,64,512]{2,1,0:T(8,128)} fusion(f32[30,64,512]{2,1,0:T(8,128)S(1)} %copy-done.1, f32[30,66,514]{2,1,0:T(8,128)} %subtract_multiply_fusion, f32[30,1,514]{2,1,0:T(1,128)} %collective-permute-done.12, f32[30,64,1]{2,1,0:T(8,128)} %copy.23, f32[30,64,1]{2,1,0:T(8,128)S(1)} %copy.25, f32[30,65,514]{2,1,0:T(8,128)} %copy-done.6, ...), kind=kLoop, calls=%fused_computation.169 | loop fusion | flops 20643840 | bytes 31542256 | tf_op jit(solution)/shard_map/add | solution.py:73
  457.9 55.7 %while.157 = (s32[]{:T(128)}, f32[64,512]{1,0:T(8,128)S(1)}, f32[64,512]{1,0:T(8,128)S(1)}, f32[30,64,512]{2,1,0:T(8,128)}, f32[30,64,512]{2,1,0:T(8,128)}, /*in...) while((s32[]{:T(128)}, f32[64,512]{1,0:T(8,128)S(1)}, ...), condition=%wide.region_2.3_spmd.clone, body=%wide.region_1.2_spmd.clone.sunk | while | flops 360451 | bytes 1180271 | solution.py:38
  516.1 51.8 %while.158 = (s32[]{:T(128)}, f32[64,512]{1,0:T(8,128)S(1)}, f32[30,64,512]{2,1,0:T(8,128)}, f32[30,64,512]{2,1,0:T(8,128)}, f32[30,64,512]{2,1,0:T(8,128)}, /*index=5*/s32[]{:T(128)}, s32[]{:T(128)}, s32[]{:T(128)}) while((s32[]{:T(128)}, f32[64,512]{1,0:T(8,128)S(1)}, f32[30,64,512]{2,1,0:T(8,128)}, f32[30,64,512]{2,1,0:T(8,128)}, ...), condition=%wide.region_4.5_spmd.clone, body=%wide.region_3.4_spmd.clone.sunk | while | flops 98308 | bytes 655471 | solution.py:45
  567.9 5.3 select_reduce_fusion.1
  573.5 15.9 %fusion.70 = f32[30,64,512]{2,1,0:T(8,128)} fusion(f32[30,64,512]{2,1,0:T(8,128)S(1)} %copy-done.5, f32[30,66,514]{2,1,0:T(8,128)} %subtract_multiply_fusion, f32[30,1,514]{2,1,0:T(1,128)} %collective-permute-done.25, f32[30,64,1]{2,1,0:T(8,128)S(1)} %copy.18, f32[30,64,1]{2,1,0:T(8,128)} %copy-done.18, f32[30,65,514]{2,1,0:T(8,128)} %copy-done.11, ...), kind=kLoop, calls=%fused_computation.154 | loop fusion | flops 20643840 | bytes 31542256 | tf_op jit(solution)/shard_map/add | solution.py:74
  594.3 55.7 %while.159 = (s32[]{:T(128)}, f32[64,512]{1,0:T(8,128)S(1)}, f32[64,512]{1,0:T(8,128)S(1)}, f32[30,64,512]{2,1,0:T(8,128)}, f32[30,64,512]{2,1,0:T(8,128)}, /*in...) while((s32[]{:T(128)}, f32[64,512]{1,0:T(8,128)S(1)}, ...), condition=%wide.region_8.9_spmd.clone, body=%wide.region_7.8_spmd.clone.sunk | while | flops 360451 | bytes 1180271 | solution.py:38
  652.4 52.1 %while.160 = (s32[]{:T(128)}, f32[64,512]{1,0:T(8,128)S(1)}, f32[30,64,512]{2,1,0:T(8,128)}, f32[30,64,512]{2,1,0:T(8,128)}, f32[30,64,512]{2,1,0:T(8,128)}, /*index=5*/s32[]{:T(128)}, s32[]{:T(128)}, s32[]{:T(128)}) while((s32[]{:T(128)}, f32[64,512]{1,0:T(8,128)S(1)}, f32[30,64,512]{2,1,0:T(8,128)}, f32[30,64,512]{2,1,0:T(8,128)}, ...), condition=%wide.region_10.11_spmd.clone, body=%wide.region_9.10_spmd.clone.sunk | while | flops 98308 | bytes 655471 | solution.py:45
  704.6 4.5 select_reduce_fusion
  709.4 467.3 %while.165 = (s32[]{:T(128)}, f32[64,512]{1,0:T(8,128)S(1)}, f32[64,512]{1,0:T(8,128)S(1)}, f32[64,512]{1,0:T(8,128)S(1)}, f32[64,512]{1,0:T(8,128)S(1)}, /*inde...) while((s32[]{:T(128)}, f32[64,512]{1,0:T(8,128)S(1)}, ...), condition=%wide.region_14.15_spmd.clone.clone.clone, body=%wide.region_13.14_spmd.clone.clone.clone.sunk | while | flops 1774400 | bytes 6826272 | solution.py:150
  727.3 3.6 collective-permute-done
  742.4 3.6 collective-permute-done
  773.6 3.6 collective-permute-done
  789.7 3.6 collective-permute-done
  804.8 3.6 collective-permute-done
  820.9 3.6 collective-permute-done
  835.9 3.6 collective-permute-done
  852.1 3.6 collective-permute-done
  1176.8 8.4 add_select_fusion
  (954 shorter events, 971.9 us)
Async XLA Ops:
  1.5 33.8 %collective-permute-start.23 = (s32[64,1]{1,0:T(8,128)S(1)}, s32[64,1]{1,0:T(8,128)S(1)}, u32[]{:S(2)}, u32[]{:S(2)}) collective-permute-start(s32[64,1]{1,0:T(8,128)S(1)} %get-tuple-element.1216), channel_id=1, source_target_pairs={{0,2},{2,4},{4,6},{6,0},{1,3},{3,5},{5,7},{7,1}} | collective-permute-start | bytes 776 | tf_op jit(solution)/shard_map/ppermute | solution.py:126
  4.9 31.5 %collective-permute-start.5 = (s32[64,1]{1,0:T(8,128)S(1)}, s32[64,1]{1,0:T(8,128)S(1)}, u32[]{:S(2)}, u32[]{:S(2)}) collective-permute-start(s32[64,1]{1,0:T(8,128)S(1)} %get-tuple-element.1217), channel_id=1, source_target_pairs={{0,6},{2,0},{4,2},{6,4},{1,7},{3,1},{5,3},{7,5}} | collective-permute-start | bytes 776 | tf_op jit(solution)/shard_map/ppermute | solution.py:127
  8.7 49.4 %collective-permute-start.6 = (f32[30,64,1]{1,2,0:T(1,128)}, f32[30,64,1]{1,2,0:T(1,128)}, u32[]{:S(2)}, u32[]{:S(2)}) collective-permute-start(f32[30,64,1]{1,2,0:T(1,128)} %copy.41), channel_id=1, source_target_pairs={{0,6},{2,0},{4,2},{6,4},{1,7},{3,1},{5,3},{7,5}} | collective-permute-start | bytes 23048 | tf_op jit(solution)/shard_map/ppermute | solution.py:127
  11.6 50.1 %collective-permute-start.7 = (f32[30,64,1]{1,2,0:T(1,128)}, f32[30,64,1]{1,2,0:T(1,128)}, u32[]{:S(2)}, u32[]{:S(2)}) collective-permute-start(f32[30,64,1]{1,2,0:T(1,128)} %copy.42), channel_id=1, source_target_pairs={{0,2},{2,4},{4,6},{6,0},{1,3},{3,5},{5,7},{7,1}} | collective-permute-start | bytes 23048 | tf_op jit(solution)/shard_map/ppermute | solution.py:126
  36.4 29.5 %collective-permute-start.13 = (f32[30,64,1]{1,2,0:T(1,128)}, f32[30,64,1]{1,2,0:T(1,128)S(1)}, u32[]{:S(2)}, u32[]{:S(2)}) collective-permute-start(f32[30,64,1]{1,2,0:T(1,128)} %copy.45), channel_id=1, source_target_pairs={{0,2},{2,4},{4,6},{6,0},{1,3},{3,5},{5,7},{7,1}} | collective-permute-start | bytes 23048 | tf_op jit(solution)/shard_map/ppermute | solution.py:126
  40.3 16.9 %collective-permute-start.26 = (s32[1,514]{1,0:T(1,128)S(1)}, s32[1,514]{1,0:T(1,128)S(1)}, u32[]{:S(2)}, u32[]{:S(2)}) collective-permute-start(s32[1,514]{1,0:T(1,128)S(1)} %get-tuple-element.1204), channel_id=1, source_target_pairs={{0,1},{2,3},{4,5},{6,7}} | collective-permute-start | bytes 6176 | tf_op jit(solution)/shard_map/ppermute | solution.py:129
  55.2 13.1 %collective-permute-start.14 = (f32[30,64,1]{1,2,0:T(1,128)S(1)}, f32[30,64,1]{1,2,0:T(1,128)S(1)}, u32[]{:S(2)}, u32[]{:S(2)}) collective-permute-start(f32[30,64,1]{1,2,0:T(1,128)S(1)} %copy-done.46), channel_id=1, source_target_pairs={{0,6},{2,0},{4,2},{6,4},{1,7},{3,1},{5,3},{7,5}} | collective-permute-start | bytes 23048 | tf_op jit(solution)/shard_map/ppermute | solution.py:127
  58.1 24.8 %collective-permute-start.10 = (f32[30,64,1]{1,2,0:T(1,128)S(1)}, f32[30,64,1]{1,2,0:T(1,128)}, u32[]{:S(2)}, u32[]{:S(2)}) collective-permute-start(f32[30,64,1]{1,2,0:T(1,128)S(1)} %copy.44), channel_id=1, source_target_pairs={{0,2},{2,4},{4,6},{6,0},{1,3},{3,5},{5,7},{7,1}} | collective-permute-start | bytes 23048 | tf_op jit(solution)/shard_map/ppermute | solution.py:126
  59.2 14.2 %collective-permute-start.17 = (f32[30,64,1]{1,2,0:T(1,128)S(1)}, f32[30,64,1]{1,2,0:T(1,128)S(1)}, u32[]{:S(2)}, u32[]{:S(2)}) collective-permute-start(f32[30,64,1]{1,2,0:T(1,128)S(1)} %copy-done.47), channel_id=1, source_target_pairs={{0,2},{2,4},{4,6},{6,0},{1,3},{3,5},{5,7},{7,1}} | collective-permute-start | bytes 23048 | tf_op jit(solution)/shard_map/ppermute | solution.py:126
  65.5 12.9 %collective-permute-start.18 = (f32[30,64,1]{1,2,0:T(1,128)S(1)}, f32[30,64,1]{1,2,0:T(1,128)S(1)}, u32[]{:S(2)}, u32[]{:S(2)}) collective-permute-start(f32[30,64,1]{1,2,0:T(1,128)S(1)} %copy-done.45), channel_id=1, source_target_pairs={{0,6},{2,0},{4,2},{6,4},{1,7},{3,1},{5,3},{7,5}} | collective-permute-start | bytes 23048 | tf_op jit(solution)/shard_map/ppermute | solution.py:127
  66.3 18.9 %collective-permute-start.9 = (f32[30,64,1]{1,2,0:T(1,128)}, f32[30,64,1]{1,2,0:T(1,128)}, u32[]{:S(2)}, u32[]{:S(2)}) collective-permute-start(f32[30,64,1]{1,2,0:T(1,128)} %copy.43), channel_id=1, source_target_pairs={{0,6},{2,0},{4,2},{6,4},{1,7},{3,1},{5,3},{7,5}} | collective-permute-start | bytes 23048 | tf_op jit(solution)/shard_map/ppermute | solution.py:127
  72.1 637.1 %collective-permute-start.22 = (f32[1,514]{1,0:T(1,128)S(1)}, f32[1,514]{1,0:T(1,128)S(1)}, u32[]{:S(2)}, u32[]{:S(2)}) collective-permute-start(f32[1,514]{1,0:T(1,128)S(1)} %pad_maximum_fusion.52), channel_id=1, source_target_pairs={{1,0},{3,2},{5,4},{7,6}} | collective-permute-start | bytes 6176 | tf_op jit(solution)/shard_map/ppermute | solution.py:130
  74.8 19.3 %collective-permute-start.8 = (f32[30,1,514]{2,1,0:T(1,128)}, f32[30,1,514]{2,1,0:T(1,128)}, u32[]{:S(2)}, u32[]{:S(2)}) collective-permute-start(f32[30,1,514]{2,1,0:T(1,128)} %get-tuple-element.1183), channel_id=1, source_target_pairs={{0,1},{2,3},{4,5},{6,7}} | collective-permute-start | bytes 185048 | tf_op jit(solution)/shard_map/ppermute | solution.py:129
  81.5 17.2 %collective-permute-start.15 = (f32[30,1,514]{2,1,0:T(1,128)}, f32[30,1,514]{2,1,0:T(1,128)S(1)}, u32[]{:S(2)}, u32[]{:S(2)}) collective-permute-start(f32[30,1,514]{2,1,0:T(1,128)} %get-tuple-element.1188), channel_id=1, source_target_pairs={{0,1},{2,3},{4,5},{6,7}} | collective-permute-start | bytes 185048 | tf_op jit(solution)/shard_map/ppermute | solution.py:129
  83.9 16.1 %collective-permute-start.16 = (f32[30,1,514]{2,1,0:T(1,128)}, f32[30,1,514]{2,1,0:T(1,128)S(1)}, u32[]{:S(2)}, u32[]{:S(2)}) collective-permute-start(f32[30,1,514]{2,1,0:T(1,128)} %get-tuple-element.1189), channel_id=1, source_target_pairs={{1,0},{3,2},{5,4},{7,6}} | collective-permute-start | bytes 185048 | tf_op jit(solution)/shard_map/ppermute | solution.py:130
  89.9 139.8 %collective-permute-start.19 = (f32[30,1,514]{2,1,0:T(1,128)}, f32[30,1,514]{2,1,0:T(1,128)}, u32[]{:S(2)}, u32[]{:S(2)}) collective-permute-start(f32[30,1,514]{2,1,0:T(1,128)} %get-tuple-element.1186), channel_id=1, source_target_pairs={{0,1},{2,3},{4,5},{6,7}} | collective-permute-start | bytes 185048 | tf_op jit(solution)/shard_map/ppermute | solution.py:129
  97.4 133.6 %collective-permute-start.20 = (f32[30,1,514]{2,1,0:T(1,128)}, f32[30,1,514]{2,1,0:T(1,128)}, u32[]{:S(2)}, u32[]{:S(2)}) collective-permute-start(f32[30,1,514]{2,1,0:T(1,128)} %get-tuple-element.1187), channel_id=1, source_target_pairs={{1,0},{3,2},{5,4},{7,6}} | collective-permute-start | bytes 185048 | tf_op jit(solution)/shard_map/ppermute | solution.py:130
  98.7 332.5 %collective-permute-start.11 = (f32[30,1,514]{2,1,0:T(1,128)}, f32[30,1,514]{2,1,0:T(1,128)}, u32[]{:S(2)}, u32[]{:S(2)}) collective-permute-start(f32[30,1,514]{2,1,0:T(1,128)} %get-tuple-element.1184), channel_id=1, source_target_pairs={{1,0},{3,2},{5,4},{7,6}} | collective-permute-start | bytes 185048 | tf_op jit(solution)/shard_map/ppermute | solution.py:130
  224.9 210.6 %collective-permute-start.12 = (f32[30,1,514]{2,1,0:T(1,128)}, f32[30,1,514]{2,1,0:T(1,128)}, u32[]{:S(2)}, u32[]{:S(2)}) collective-permute-start(f32[30,1,514]{2,1,0:T(1,128)} %get-tuple-element.1185), channel_id=1, source_target_pairs={{0,1},{2,3},{4,5},{6,7}} | collective-permute-start | bytes 185048 | tf_op jit(solution)/shard_map/ppermute | solution.py:129
  229.8 343.5 %collective-permute-start.25 = (f32[30,1,514]{2,1,0:T(1,128)}, f32[30,1,514]{2,1,0:T(1,128)}, u32[]{:S(2)}, u32[]{:S(2)}) collective-permute-start(f32[30,1,514]{2,1,0:T(1,128)} %get-tuple-element.1182), channel_id=1, source_target_pairs={{1,0},{3,2},{5,4},{7,6}} | collective-permute-start | bytes 185048 | tf_op jit(solution)/shard_map/ppermute | solution.py:130
  802.9 8.1 collective-permute-start.1
  834.0 8.3 collective-permute-start.1
  865.1 8.3 collective-permute-start.1
  896.3 8.3 collective-permute-start.1
  927.5 8.3 collective-permute-start.1
  958.7 8.3 collective-permute-start.1
  989.9 8.3 collective-permute-start.1
  1021.0 8.3 collective-permute-start.1
  1052.2 8.3 collective-permute-start.1
  1083.4 8.3 collective-permute-start.1
  1114.6 8.3 collective-permute-start.1
  1145.7 8.3 collective-permute-start.1
  (162 other events, 1164.2 us)
where the time goes:
time: 1200 us; the launch traced here: 1190 us
  other arithmetic  678 us (56%)
  starting transfers between devices  233 us (19%)
  waiting for transfers between devices  180 us (15%)
  local copies, waits for them, and re-layouts  89.3 us (7%)
    dynamic_update_slice x240, other arithmetic, tri_solve(): lax.scan(down, start, (low_links, up_links, right_side))  430 us
    ppermute x36, waiting for transfers between devices, exchange(): from_east = lax.ppermute(field[..., :1], 'col', west_moves)  109 us
    ppermute x35, starting transfers between devices, exchange(): from_south = lax.ppermute(wide[..., -1:, :], 'row', north_moves)  108 us
    ppermute x36, waiting for transfers between devices, exchange(): from_west = lax.ppermute(field[..., -1:], 'col', east_moves)  65.8 us
    another operation x1, other arithmetic, ocean_columns(): jnp.cumsum(density, axis=0) - 0.5 * density  65.6 us
    ppermute x36, starting transfers between devices, exchange(): from_west = lax.ppermute(field[..., -1:], 'col', east_moves)  64.5 us
    ppermute x36, starting transfers between devices, exchange(): from_north = lax.ppermute(wide[..., :1, :], 'row', south_moves)  46.5 us
    sub x2, other arithmetic, advect(): tracer_mid - 0.5 * TIME_STEP * (flux_east - flux_west + flux_north - flux...  29.6 us
  transfers between devices with their start and end apart: 143, of which 91 were waited for; matrix products, arithmetic and copies ran while one was open for 57% of the time, Pallas kernels for 0%

commit v1 on v0

v1 whole, which is shorter than its diff:
```python
import functools

import jax
import jax.numpy as jnp
from jax import lax
from jax.experimental import pallas as pl
from jax.experimental.pallas import tpu as pltpu
from jax.sharding import PartitionSpec as P

TIME_STEP = 1.0
GRAVITY = 16.0
BC_GRAVITY = 4.0
EXPAND_T = 0.2
CONTRACT_S = 0.6
CORIO_F0 = 0.4
CORIO_BETA = 0.4
VISC_R = 2.0
DIFF_R = 0.5

MESH = pl.DeviceIdType.MESH
SL = 8
LN = 128
LEVELS = 30
NR = 64
NC = 4
HY = 32
HX = 32
EXT = NR + HY
PAD = SL
EROWS = EXT + 2 * PAD
STRIPS = EXT // SL
LANE_COUNT = 4 * LEVELS
LANE_DEPTH = LANE_COUNT + 1


def elimination(strength):
    pivots, ends = [], []
    for level in range(LEVELS):
        below = strength * strength / pivots[-1] if level else strength
        pivots.append(1.0 + 2.0 * strength - below)
        ends.append(1.0 + strength - below)
    inverse = [1.0 / pivot for pivot in pivots]
    carry = [strength / pivot for pivot in pivots]
    ending = [pivot / end for pivot, end in zip(pivots, ends)]
    return inverse, carry, ending


INV_V, CARRY_V, END_V = elimination(VISC_R)
INV_D, CARRY_D, END_D = elimination(DIFF_R)


def roll_e(x):
    return pltpu.roll(x, 127, x.ndim - 1)


def roll_w(x):
    return pltpu.roll(x, 1, x.ndim - 1)


def turn(x, amount):
    amount = amount % LN
    return pltpu.roll(x, amount, x.ndim - 1) if amount else x


def following(x):
    return jnp.concatenate([x[1:], x[:1]], axis=0)


def preceding(x):
    return jnp.concatenate([x[-1:], x[:-1]], axis=0)


def step_kernel(n_col, wts, u_h, v_h, t_h, s_h, eta_h, tu_h, tv_h, dep_h, cnt_h,
                vu, vv, vt, vs, aux,
                ub, vb, tb, sb, eta, ua, ubt, va, vbt, dep, cnt, cnt_i, fx, fy,
                au, av, bu, bv, cu, cv, mu, mv, accu, accv, meanu, meanv,
                pk, pkl, rx, rxl,
                sem_in, sem_2d, sem_rs, sem_rr, sem_fs, sem_fr, sem_xs, sem_xr, sem_ls, sem_lr, sem_gs, sem_gr):
    col = lax.axis_index('col')
    row = lax.axis_index('row')
    east = lax.rem(col + 1, n_col)
    west = lax.rem(col + n_col - 1, n_col)
    other = 1 - row
    own = pl.multiple_of(PAD + HY * row, SL)
    near = pl.multiple_of(HY * other, SL)
    far = pl.multiple_of(PAD + NR * row, SL)
    mid = PAD + HY
    lane = lax.broadcasted_iota(jnp.int32, (SL, LN), 1)
    sub = lax.broadcasted_iota(jnp.int32, (SL, LN), 0)
    cubes = ((u_h, ub), (v_h, vb), (t_h, tb), (s_h, sb))
    flats = ((eta_h, eta), (tu_h, ua), (tv_h, va), (dep_h, dep), (cnt_h, cnt_i))

    loads = {}
    for c in (0, 3, 1, 2):
        for f, (src, dst) in enumerate(cubes):
            loads[f, c] = pltpu.make_async_copy(
                src.at[:, :, pl.ds(c * LN, LN)], dst.at[:, c, pl.ds(SL, NR), :], sem_in.at[f, c])
    flat_loads = []
    for f, (src, dst) in enumerate(flats):
        for c in range(NC):
            flat_loads.append(pltpu.make_async_copy(
                src.at[:, pl.ds(c * LN, LN)], dst.at[c, pl.ds(own, NR), :], sem_2d.at[f, c]))
    for c in (0, 3):
        for f in range(4):
            loads[f, c].start()
    for copy in flat_loads:
        copy.start()
    for c in (1, 2):
        for f in range(4):
            loads[f, c].start()

    barrier = pltpu.get_barrier_semaphore()
    for peer in ({'col': east, 'row': row}, {'col': west, 'row': row}, {'col': col, 'row': other},
                 {'col': east, 'row': other}, {'col': west, 'row': other}):
        pl.semaphore_signal(barrier, inc=1, device_id=peer, device_id_type=MESH)

    wall = pl.multiple_of((NR + SL) * row, SL)
    zero4 = jnp.zeros((NC, SL, LN), jnp.float32)

    @pl.loop(0, LEVELS)
    def _(k):
        for _, dst in cubes:
            dst[k, 0:NC, pl.ds(wall, SL), :] = zero4

    zero5 = jnp.zeros((NC + 1, SL, LN), jnp.float32)
    for start in (0, PAD + EXT):
        for ref in (eta, ua, ubt, va, vbt, dep, cnt, fx, fy):
            ref[:, pl.ds(start, SL), :] = zero5
        cnt_i[:, pl.ds(start, SL), :] = jnp.zeros((NC, SL, LN), jnp.int32)
        for d in range(2):
            for p in range(2):
                rx[d, p, pl.ds(start, SL), :] = jnp.zeros((SL, LN), jnp.float32)

    pl.semaphore_wait(barrier, 5)

    row_copies = []
    edge_src = pl.multiple_of((NR - SL) * other, SL)
    for f, (src, dst) in enumerate(cubes):
        for c in range(NC):
            row_copies.append(pltpu.make_async_remote_copy(
                src_ref=src.at[:, pl.ds(edge_src, SL), pl.ds(c * LN, LN)],
                dst_ref=dst.at[:, c, pl.ds(wall, SL), :],
                send_sem=sem_rs.at[f, c], recv_sem=sem_rr.at[f, c],
                device_id={'col': col, 'row': other}, device_id_type=MESH))
    flat_copies = []
    for f, (src, dst) in enumerate(flats):
        for c in range(NC):
            flat_copies.append(pltpu.make_async_remote_copy(
                src_ref=src.at[pl.ds(near, HY), pl.ds(c * LN, LN)],
                dst_ref=dst.at[c, pl.ds(far, HY), :],
                send_sem=sem_fs.at[f, c], recv_sem=sem_fr.at[f, c],
                device_id={'col': col, 'row': other}, device_id_type=MESH))
    for copy in row_copies + flat_copies:
        copy.start()

    zero1 = jnp.zeros((SL, LN), jnp.float32)
    for f, (_, buf) in enumerate(cubes):
        loads[f, 0].wait()
        loads[f, 3].wait()

        @pl.loop(0, NR // 16)
        def _(q):
            for half_q in range(2):
                r = 2 * q + half_q
                rows = pl.ds(pl.multiple_of(SL + SL * r, SL), SL)
                rows_o = pl.ds(pl.multiple_of(SL * r, SL), SL)
                acc_e = zero1 if f == 0 else pk[0, 0, rows_o, :]
                acc_w = zero1 if f == 0 else pk[1, 0, rows_o, :]
                for k in range(LEVELS):
                    m = f * LEVELS + k
                    acc_e = jnp.where(lane == (m - 1) % LN, turn(buf[k, NC - 1, rows, :], m), acc_e)
                    acc_w = jnp.where(lane == m, turn(buf[k, 0, rows, :], m), acc_w)
                pk[0, 0, rows_o, :] = acc_e
                pk[1, 0, rows_o, :] = acc_w

    for copy in flat_loads:
        copy.wait()

    @pl.loop(0, NR // SL)
    def _(r):
        rows_e = pl.ds(pl.multiple_of(own + SL * r, SL), SL)
        rows_o = pl.ds(pl.multiple_of(SL * r, SL), SL)
        acc_e = pk[0, 0, rows_o, :]
        acc_w = pk[1, 0, rows_o, :]
        for m, ref in ((LANE_COUNT, cnt_i), (LANE_DEPTH, dep)):
            acc_e = jnp.where(lane == m - 1, turn(ref[NC - 1, rows_e, :].astype(jnp.float32), m), acc_e)
            acc_w = jnp.where(lane == m, turn(ref[0, rows_e, :].astype(jnp.float32), m), acc_w)
        pk[0, 0, rows_o, :] = acc_e
        pk[1, 0, rows_o, :] = acc_w
        acc_e = turn(eta[NC - 1, rows_e, :], HX)
        acc_w = eta[0, rows_e, :]
        for p, ref in ((1, ua), (2, va), (3, dep)):
            here = lane >= p * HX
            acc_e = jnp.where(here, turn(ref[NC - 1, rows_e, :], HX * (p + 1)), acc_e)
            acc_w = jnp.where(here, turn(ref[0, rows_e, :], HX * p), acc_w)
        pk[0, 1, rows_o, :] = acc_e
        pk[1, 1, rows_o, :] = acc_w

    for copy in flat_copies:
        copy.wait_recv()
    for r in range(STRIPS):
        cnt[0:NC, pl.ds(PAD + SL * r, SL), :] = cnt_i[:, pl.ds(PAD + SL * r, SL), :].astype(jnp.float32)

    x_copies = []
    for d, side in ((0, east), (1, west)):
        x_copies.append(pltpu.make_async_remote_copy(
            src_ref=pk.at[d], dst_ref=rx.at[d, :, pl.ds(own, NR), :],
            send_sem=sem_xs.at[d, 0], recv_sem=sem_xr.at[d, 0],
            device_id={'col': side, 'row': row}, device_id_type=MESH))
        x_copies.append(pltpu.make_async_remote_copy(
            src_ref=pk.at[d, :, pl.ds(near, HY), :], dst_ref=rx.at[d, :, pl.ds(far, HY), :],
            send_sem=sem_xs.at[d, 1], recv_sem=sem_xr.at[d, 1],
            device_id={'col': side, 'row': other}, device_id_type=MESH))
    for copy in x_copies:
        copy.start()

    for c in (1, 2):
        for f in range(4):
            loads[f, c].wait()
    for copy in row_copies:
        copy.wait_recv()

    half = 0.5 * BC_GRAVITY / LEVELS
    first0 = lax.broadcasted_iota(jnp.int32, (1, SL, LN), 2) == 0
    last127 = lax.broadcasted_iota(jnp.int32, (1, SL, LN), 2) == 127

    def shift_e(mine, following_tile):
        return roll_e(jnp.where(first0, following_tile, mine))

    def shift_w(mine, preceding_tile):
        return roll_w(jnp.where(last127, preceding_tile, mine))

    def ring_e(x):
        return shift_e(x, following(x))

    def ring_w(x):
        return shift_w(x, preceding(x))

    def inner(x):
        return x[1:3], x[2:4], x[0:2]

    def outer(x):
        return (jnp.concatenate([x[0:1], x[3:4]], axis=0), jnp.concatenate([x[1:2], x[4:5]], axis=0),
                jnp.concatenate([x[4:5], x[2:3]], axis=0))

    def every(x):
        return x[0:4], x[1:5], jnp.concatenate([x[4:5], x[0:3]], axis=0)

    def momentum(r, tiles, places):
        rb = pl.multiple_of(SL + SL * r, SL)
        eb = pl.multiple_of(own + SL * r, SL)
        out = pl.ds(pl.multiple_of(SL * r, SL), SL)
        y = (NR * row + SL * r + sub).astype(jnp.float32)
        fu4 = 0.25 * (CORIO_F0 + CORIO_BETA * ((y + 0.5) / (2 * NR) - 0.5))
        fv4 = 0.25 * (CORIO_F0 + CORIO_BETA * ((y + 1.0) / (2 * NR) - 0.5))

        def load(ref, k, dr=0):
            return ref[k, :, pl.ds(rb + dr, SL), :]

        def put(ref, rows, value):
            for i, c in enumerate(places):
                ref[c, rows, :] = value[i]

        count, count_e, _ = tiles(cnt[:, pl.ds(eb, SL), :])
        lu = jnp.minimum(count, shift_e(count, count_e))
        lv = jnp.minimum(count, tiles(cnt[:, pl.ds(eb + 1, SL), :])[0])
        qx = qy = su = sv = sdu = sdv = jnp.zeros((len(places), SL, LN), jnp.float32)
        wu = wv = None
        for k in range(LEVELS):
            u, ue, uw = tiles(load(ub, k))
            un, _, unw = tiles(load(ub, k, 1))
            us = tiles(load(ub, k, -1))[0]
            v, ve, vw = tiles(load(vb, k))
            vn = tiles(load(vb, k, 1))[0]
            vso, vse, _ = tiles(load(vb, k, -1))
            s0, s_e, _ = tiles(load(sb, k))
            t0, t_e, _ = tiles(load(tb, k))
            rho = (CONTRACT_S * half) * s0 - (EXPAND_T * half) * t0
            rho_e = (CONTRACT_S * half) * s_e - (EXPAND_T * half) * t_e
            rho_n = (CONTRACT_S * half) * tiles(load(sb, k, 1))[0] - (EXPAND_T * half) * tiles(load(tb, k, 1))[0]
            w2 = v + vso
            w4 = w2 + shift_e(w2, ve + vse)
            y2 = u + un
            y4 = y2 + shift_w(y2, uw + unw)
            dx = shift_e(rho, rho_e) - rho
            dy = rho_n - rho
            px = qx + dx
            qx = px + dx
            py = qy + dy
            qy = py + dy
            du = w4 * (fu4 - 0.125 * (un - us)) - (0.5 * u) * (shift_e(u, ue) - shift_w(u, uw)) - px
            dv = -(y4 * (fv4 + 0.125 * (shift_e(v, ve) - shift_w(v, vw))) + (0.5 * v) * (vn - vso) + py)
            on_u = lu > float(k)
            on_v = lv > float(k)
            su = su + jnp.where(on_u, u, 0.0)
            sv = sv + jnp.where(on_v, v, 0.0)
            sdu = sdu + jnp.where(on_u, du, 0.0)
            sdv = sdv + jnp.where(on_v, dv, 0.0)
            tu, tv = u + du, v + dv
            wu = INV_V[k] * (tu if k == 0 else tu + VISC_R * wu)
            wv = INV_V[k] * (tv if k == 0 else tv + VISC_R * wv)
            put(vu.at[k], out, wu)
            put(vv.at[k], out, wv)
        inv_u = 1.0 / jnp.maximum(lu, 1.0)
        inv_v = 1.0 / jnp.maximum(lv, 1.0)
        depth, depth_e, _ = tiles(dep[:, pl.ds(eb, SL), :])
        hu = 0.5 * (depth + shift_e(depth, depth_e))
        hv = 0.5 * (depth + tiles(dep[:, pl.ds(eb + 1, SL), :])[0])
        put(fx, pl.ds(eb, SL), hu * (sdu * inv_u) / TIME_STEP)
        put(fy, pl.ds(eb, SL), hv * (sdv * inv_v) / TIME_STEP)
        put(meanu, out, (su + sdu) * inv_u)
        put(meanv, out, (sv + sdv) * inv_v)
        put(aux.at[0], out, count)
        put(aux.at[1], out, lu)
        put(aux.at[2], out, lv)

    def tracers(r):
        rb = pl.multiple_of(SL + SL * r, SL)
        eb = pl.multiple_of(own + SL * r, SL)
        out = pl.ds(pl.multiple_of(SL * r, SL), SL)

        def load(ref, k, dr=0):
            return ref[k, :, pl.ds(rb + dr, SL), :]

        count, count_e, count_w = every(cnt[:, pl.ds(eb, SL), :])
        lu = jnp.minimum(count, shift_e(count, count_e))
        luw = jnp.minimum(count, shift_w(count, count_w))
        lv = jnp.minimum(count, cnt[0:NC, pl.ds(eb + 1, SL), :])
        lvs = jnp.minimum(count, cnt[0:NC, pl.ds(eb - 1, SL), :])
        half_dt = 0.5 * TIME_STEP
        carried = [None, None]
        for k in range(LEVELS):
            level = float(k)
            u, _, uw = every(load(ub, k))
            ge = jnp.where(lu > level, half_dt * u, 0.0)
            gw = jnp.where(luw > level, half_dt * shift_w(u, uw), 0.0)
            gn = jnp.where(lv > level, half_dt * load(vb, k)[:NC], 0.0)
            gs = jnp.where(lvs > level, half_dt * load(vb, k, -1)[:NC], 0.0)
            keep = 1.0 - (ge - gw + gn - gs)
            inside = count > level
            for i, (buf, dst) in enumerate(((tb, vt), (sb, vs))):
                q, qe, qw = every(load(buf, k))
                new = keep * q - (ge * shift_e(q, qe) - gw * shift_w(q, qw)
                                  + gn * load(buf, k, 1)[:NC] - gs * load(buf, k, -1)[:NC])
                w = INV_D[k] * (new if k == 0 else new + DIFF_R * carried[i])
                carried[i] = w
                dst[k, :, out, :] = jnp.where(inside, w, new)

    @pl.loop(0, NR // SL)
    def _(r):
        momentum(r, inner, (1, 2))

    for copy in x_copies:
        copy.wait_recv()

    even = lax.rem(lane, 2) == 0

    def unpack(r):
        eb = pl.multiple_of(own + SL * r, SL)
        from_west, from_east = rx[0, 0, pl.ds(eb, SL), :], rx[1, 0, pl.ds(eb, SL), :]
        return jnp.where(even, from_east, from_west), jnp.where(even, from_west, from_east)

    @pl.loop(0, NR // SL + 2)
    def _(q):
        r = q - 1
        merged = unpack(r)
        rows = pl.ds(pl.multiple_of(SL * q, SL), SL)
        for f, (_, buf) in enumerate(cubes):
            for k in range(LEVELS):
                m = f * LEVELS + k
                buf[k, NC, rows, :] = turn(merged[m % 2], -m)
        rows = pl.ds(pl.multiple_of(own + SL * r, SL), SL)
        cnt[NC, rows, :] = turn(merged[LANE_COUNT % 2], -LANE_COUNT)
        dep[NC, rows, :] = turn(merged[LANE_DEPTH % 2], -LANE_DEPTH)

    @pl.loop(0, NR // SL)
    def _(r):
        momentum(r, outer, (0, 3))

    for r in range(NR // SL):
        rows_e = pl.ds(pl.multiple_of(own + SL * r, SL), SL)
        acc_e = turn(fx[NC - 1, rows_e, :], HX)
        acc_w = fx[0, rows_e, :]
        for p, ref in ((1, fy), (2, cnt)):
            here = lane >= p * HX
            acc_e = jnp.where(here, turn(ref[NC - 1, rows_e, :], HX * (p + 1)), acc_e)
            acc_w = jnp.where(here, turn(ref[0, rows_e, :], HX * p), acc_w)
        pkl[0, pl.ds(SL * r, SL), :] = acc_e
        pkl[1, pl.ds(SL * r, SL), :] = acc_w

    late = []
    for f, ref in enumerate((fx, fy)):
        late.append(pltpu.make_async_remote_copy(
            src_ref=ref.at[pl.ds(0, NC), pl.ds(mid, HY), :], dst_ref=ref.at[pl.ds(0, NC), pl.ds(far, HY), :],
            send_sem=sem_gs.at[f], recv_sem=sem_gr.at[f],
            device_id={'col': col, 'row': other}, device_id_type=MESH))
    for d, side in ((0, east), (1, west)):
        late.append(pltpu.make_async_remote_copy(
            src_ref=pkl.at[d], dst_ref=rxl.at[d, pl.ds(own, NR), :],
            send_sem=sem_ls.at[d, 0], recv_sem=sem_lr.at[d, 0],
            device_id={'col': side, 'row': row}, device_id_type=MESH))
        late.append(pltpu.make_async_remote_copy(
            src_ref=pkl.at[d, pl.ds(near, HY), :], dst_ref=rxl.at[d, pl.ds(far, HY), :],
            send_sem=sem_ls.at[d, 1], recv_sem=sem_lr.at[d, 1],
            device_id={'col': side, 'row': other}, device_id_type=MESH))
    for copy in late:
        copy.start()

    @pl.loop(0, NR // SL)
    def _(r):
        tracers(r)

    for copy in late:
        copy.wait_recv()

    def strip(r, dr=0):
        return pl.ds(PAD + SL * r + dr, SL)

    for r in range(STRIPS):
        for p, ref, src in ((0, eta, 1), (1, ua, 1), (2, va, 1), (3, dep, 1), (0, fx, 2), (1, fy, 2), (2, cnt, 2)):
            from_east = rx[1, 1, strip(r), :] if src == 1 else rxl[1, strip(r), :]
            from_west = rx[0, 1, strip(r), :] if src == 1 else rxl[0, strip(r), :]
            ref[NC, strip(r), :] = jnp.where(
                lane < HX, turn(from_east, -HX * p),
                jnp.where(lane >= LN - HX, turn(from_west, LN - HX - HX * p), 0.0))

    dt_fast = TIME_STEP / LEVELS
    for r in range(STRIPS):
        y = (HY * row + SL * r + sub).astype(jnp.float32)
        f_u = CORIO_F0 + CORIO_BETA * ((y + 0.5) / (2 * NR) - 0.5)
        f_v = CORIO_F0 + CORIO_BETA * ((y + 1.0) / (2 * NR) - 0.5)
        rows = strip(r)
        count, depth = cnt[:, rows, :], dep[:, rows, :]
        wet_u = (jnp.minimum(count, ring_e(count)) > 0.0).astype(jnp.float32)
        wet_v = (jnp.minimum(count, cnt[:, strip(r, 1), :]) > 0.0).astype(jnp.float32)
        mu[:, rows, :] = wet_u
        mv[:, rows, :] = wet_v
        au[:, rows, :] = wet_u * (0.25 * dt_fast * f_u)
        av[:, rows, :] = wet_v * (0.25 * dt_fast * f_v)
        bu[:, rows, :] = wet_u * (dt_fast * dt_fast) * fx[:, rows, :]
        bv[:, rows, :] = wet_v * (dt_fast * dt_fast) * fy[:, rows, :]
        scale = 0.5 * GRAVITY * dt_fast * dt_fast
        cu[:, rows, :] = wet_u * (scale * (depth + ring_e(depth)))
        cv[:, rows, :] = wet_v * (scale * (depth + dep[:, strip(r, 1), :]))
        ua[:, rows, :] = dt_fast * ua[:, rows, :]
        va[:, rows, :] = dt_fast * va[:, rows, :]
        accu[:, pl.ds(SL * r, SL), :] = jnp.zeros((NC, SL, LN), jnp.float32)
        accv[:, pl.ds(SL * r, SL), :] = jnp.zeros((NC, SL, LN), jnp.float32)

    def subcycle(n, u_old, v_old, u_new, v_new, first):
        weight = wts[n]
        for r in range(STRIPS):
            rows = strip(r)
            u = u_old[:, rows, :]
            eta[:, rows, :] = eta[:, rows, :] - (u - ring_w(u) + v_old[:, rows, :] - v_old[:, strip(r, -1), :])
        for r in range(STRIPS):
            rows = strip(r)
            u, v, e = u_old[:, rows, :], v_old[:, rows, :], eta[:, rows, :]
            w2 = v + v_old[:, strip(r, -1), :]
            y2 = u + u_old[:, strip(r, 1), :]
            if first:
                u, v = mu[:, rows, :] * u, mv[:, rows, :] * v
            u = u + (au[:, rows, :] * (w2 + ring_e(w2)) + bu[:, rows, :] - cu[:, rows, :] * (ring_e(e) - e))
            v = v + (bv[:, rows, :] - av[:, rows, :] * (y2 + ring_w(y2)) - cv[:, rows, :] * (eta[:, strip(r, 1), :] - e))
            u_new[:, rows, :] = u
            v_new[:, rows, :] = v
            rows_a = pl.ds(SL * r, SL)
            accu[:, rows_a, :] = accu[:, rows_a, :] + weight * u[:NC]
            accv[:, rows_a, :] = accv[:, rows_a, :] + weight * v[:NC]

    subcycle(0, ua, va, ubt, vbt, True)
    subcycle(1, ubt, vbt, ua, va, False)

    @pl.loop(1, LEVELS // 2)
    def _(pair):
        subcycle(2 * pair, ua, va, ubt, vbt, False)
        subcycle(2 * pair + 1, ubt, vbt, ua, va, False)

    @pl.loop(0, NR // SL)
    def _(r):
        eb = pl.multiple_of(own + SL * r, SL)
        rows = pl.ds(eb, SL)
        rows_a = pl.ds(pl.multiple_of(eb - PAD, SL), SL)
        out = pl.ds(pl.multiple_of(SL * r, SL), SL)
        depth = dep[:, rows, :]
        hu = 0.5 * (depth + ring_e(depth))[:NC]
        hv = 0.5 * (depth + dep[:, pl.ds(eb + 1, SL), :])[:NC]
        aux[3, :, out, :] = LEVELS / TIME_STEP * accu[:, rows_a, :] / hu - meanu[:, out, :]
        aux[4, :, out, :] = LEVELS / TIME_STEP * accv[:, rows_a, :] / hv - meanv[:, out, :]
        aux[5, :, out, :] = eta[0:NC, rows, :]
        aux[6, :, out, :] = (LEVELS / TIME_STEP) * ua[0:NC, rows, :]
        aux[7, :, out, :] = (LEVELS / TIME_STEP) * va[0:NC, rows, :]

    for copy in row_copies + flat_copies + x_copies + late:
        copy.wait_send()


def finish_kernel(vu, vv, vt, vs, aux, o_eta, o_tu, o_tv, o_u, o_v, o_t, o_s):
    for c in range(NC):
        cols = pl.ds(c * LN, LN)
        o_eta[:, cols] = aux[5, c]
        o_tu[:, cols] = aux[6, c]
        o_tv[:, cols] = aux[7, c]
        count, lu, lv = aux[0, c], aux[1, c], aux[2, c]
        gu, gv = aux[3, c], aux[4, c]
        xu = xv = xt = xs = jnp.zeros((SL, LN), jnp.float32)
        for k in reversed(range(LEVELS)):
            level = float(k)
            last = count == level + 1.0
            inside = count > level
            wu, wv, wt, ws = vu[k, c], vv[k, c], vt[k, c], vs[k, c]
            xu = jnp.where(lu == level + 1.0, END_V[k] * wu, wu + CARRY_V[k] * xu)
            xv = jnp.where(lv == level + 1.0, END_V[k] * wv, wv + CARRY_V[k] * xv)
            xt = jnp.where(last, END_D[k] * wt, wt + CARRY_D[k] * xt)
            xs = jnp.where(last, END_D[k] * ws, ws + CARRY_D[k] * xs)
            o_u[k, :, cols] = jnp.where(lu > level, xu + gu, 0.0)
            o_v[k, :, cols] = jnp.where(lv > level, xv + gv, 0.0)
            o_t[k, :, cols] = jnp.where(inside, xt, wt)
            o_s[k, :, cols] = jnp.where(inside, xs, ws)


def solution(mesh):
    n_col = mesh.shape['col']

    def step(vel_u, vel_v, temperature, salinity, surf_eta, trans_u, trans_v, bottom_depth, level_count, avg_weights):
        f32 = jnp.float32
        swept = jax.ShapeDtypeStruct((LEVELS, NC, NR, LN), f32)
        vmem = pl.BlockSpec(memory_space=pltpu.VMEM)
        anywhere = pl.BlockSpec(memory_space=pl.ANY)
        wide = pltpu.VMEM((NC + 1, EROWS, LN), f32)
        cube = pltpu.VMEM((LEVELS, NC + 1, NR + 16, LN), f32)
        acc = pltpu.VMEM((NC, EXT, LN), f32)
        mean = pltpu.VMEM((NC, NR, LN), f32)
        dma = pltpu.SemaphoreType.DMA
        swept_all = pl.pallas_call(
            functools.partial(step_kernel, n_col),
            out_shape=(swept,) * 4 + (jax.ShapeDtypeStruct((SL, NC, NR, LN), f32),),
            in_specs=[pl.BlockSpec(memory_space=pltpu.SMEM)] + [anywhere] * 9,
            out_specs=(vmem,) * 5,
            scratch_shapes=[cube] * 4 + [wide] * 7 + [pltpu.VMEM((NC, EROWS, LN), jnp.int32)] + [wide] * 10
            + [acc, acc, mean, mean,
               pltpu.VMEM((2, 2, NR, LN), f32), pltpu.VMEM((2, NR, LN), f32),
               pltpu.VMEM((2, 2, EROWS, LN), f32), pltpu.VMEM((2, EROWS, LN), f32)]
            + [dma((4, NC)), dma((5, NC)), dma((4, NC)), dma((4, NC)), dma((5, NC)), dma((5, NC)),
               dma((2, 2)), dma((2, 2)), dma((2, 2)), dma((2, 2)), dma((2,)), dma((2,))],
            compiler_params=pltpu.CompilerParams(
                collective_id=0, has_side_effects=True, vmem_limit_bytes=33 * 1024 * 1024),
            name='step_kernel',
        )(avg_weights, *[pltpu.with_memory_space_constraint(x, pltpu.HBM) for x in (vel_u, vel_v, temperature, salinity, surf_eta, trans_u, trans_v, bottom_depth, level_count)])
        flat_out = jax.ShapeDtypeStruct(surf_eta.shape, f32)
        cube_out = jax.ShapeDtypeStruct(vel_u.shape, f32)
        flat_spec = pl.BlockSpec((SL, NC * LN), lambda r: (r, 0))
        cube_spec = pl.BlockSpec((LEVELS, SL, NC * LN), lambda r: (0, r, 0))
        in_spec = pl.BlockSpec((LEVELS, NC, SL, LN), lambda r: (0, 0, r, 0))
        return pl.pallas_call(
            finish_kernel,
            grid=(NR // SL,),
            out_shape=(flat_out,) * 3 + (cube_out,) * 4,
            in_specs=[in_spec] * 4 + [pl.BlockSpec((SL, NC, SL, LN), lambda r: (0, 0, r, 0))],
            out_specs=(flat_spec,) * 3 + (cube_spec,) * 4,
            compiler_params=pltpu.CompilerParams(vmem_limit_bytes=16 * 1024 * 1024),
            name='finish_kernel',
        )(*swept_all)

    cube = P(None, 'row', 'col')
    flat = P('row', 'col')
    return jax.shard_map(step, mesh=mesh, in_specs=(cube, cube, cube, cube, flat, flat, flat, flat, flat, P()), out_specs=(flat, flat, flat, cube, cube, cube, cube), check_vma=False)
```

time: 1200 us -> 51.9 us (0.04); the launches traced: 1190 us -> 51.8 us
  other arithmetic: 678 us -> 0 us
  starting transfers between devices: 233 us -> 0 us
  waiting for transfers between devices: 180 us -> 0 us
  local copies, waits for them, and re-layouts: 89.3 us -> 0.65 us
  Pallas kernels: 0 us -> 50.5 us
    dynamic_update_slice x240 -> x0, other arithmetic: 430 us -> none  [tri_solve(): lax.scan(down, start, (low_links, up_links, right_side))]
    ppermute x143 -> x0, starting transfers between devices: 233 us -> none  [the longest x35 108 us: exchange(): from_south = lax.ppermute(wide[..., -1:, :], 'row', north_moves)]
    ppermute x143 -> x0, waiting for transfers between devices: 180 us -> none  [the longest x36 109 us: exchange(): from_east = lax.ppermute(field[..., :1], 'col', west_moves)]
    add x62 -> x0, other arithmetic: 86.8 us -> none  [the longest x30 28.2 us: subcycle(): acc_u + weight * trans_u_new]
    another operation x1 -> x0, other arithmetic: 65.6 us -> none  [ocean_columns(): jnp.cumsum(density, axis=0) - 0.5 * density]
    pallas_call x0 -> x2, Pallas kernels: none -> 50.5 us  [the longest x1 41.7 us: step(): pl.pallas_call(functools.partial(step_kernel, n_col), out_shape=(swept,)...]
    sub x32 -> x0, other arithmetic: 37.7 us -> none  [the longest x2 29.6 us: advect(): tracer_mid - 0.5 * TIME_STEP * (flux_east - flux_west + flux_north - flux...]
    another operation x12 -> x0, local copies, waits for them, and re-layouts: 29.1 us -> none
  transfers between devices with their start and end apart: 143 -> 0, of which waited for: 91 -> 0; matrix products, arithmetic and copies ran while one was open for 57% -> 0% of each run, Pallas kernels for 0% -> 0%
where the time goes in v1:
time: 51.9 us; the launch traced here: 51.8 us
  Pallas kernels  50.5 us (97%)
  local copies, waits for them, and re-layouts  0.65 us (1%)
  between operations  0.65 us (1%)
    pallas_call x1, Pallas kernels, step(): pl.pallas_call(functools.partial(step_kernel, n_col), out_shape=(swept,)...  41.7 us
    pallas_call x1, Pallas kernels, step(): pl.pallas_call(finish_kernel, grid=(NR // SL,), out_shape=(flat_out,) * 3...  8.73 us

profile of v1, /device:TPU:0, one launch (start us, length us, event | category | flops | bytes accessed | tf_op | source)
XLA Modules:
  0.0 51.8 jit_solution(9507898225760053002)
XLA Ops:
  0.6 0.0 copy-start
  0.6 0.6 %copy-done = f32[30]{0:T(128)S(1)} copy-done((f32[30]{0:T(128)S(1)}, f32[30]{0:T(128)}, u32[]{:S(2)}) %copy-start) | copy-done | bytes 144
  1.3 41.7 %step_kernel.1 = (f32[30,4,64,128]{3,2,1,0:T(8,128)S(1)}, f32[30,4,64,128]{3,2,1,0:T(8,128)S(1)}, f32[30,4,64,128]{3,2,1,0:T(8,128)S(1)}, f32[30,4,64,128]{3,2,1,0:T(8,128)S(1)}, f32[8,4,64,128]{3,2,1,0:T(8,128)S(1)}) custom-call(f32[30]{0:T(128)S(1)} %copy-done, f32[30,64,512]{2,1,0:T(8,128)} %u_h.1, f32[30,64,512]{2,1,0:T(8,128)} %v_h.1, ...), custom_call_target="tpu_custom_call" | custom-call | tf_op jit(solution)/shard_map/step_kernel/pallas_call | solution.py:535
  43.0 8.7 %finish_kernel.1 = (f32[64,512]{1,0:T(8,128)}, f32[64,512]{1,0:T(8,128)}, f32[64,512]{1,0:T(8,128)}, f32[30,64,512]{2,1,0:T(8,128)}, f32[30,64,512]{2,1,0:T(8,12...) custom-call(f32[30,4,64,128]{3,2,1,0:T(8,128)S(1)} %get-tuple-element.12.vu, ...), custom_call_target="tpu_custom_call" | custom-call | tf_op jit(solution)/shard_map/finish_kernel/pallas_call | solution.py:555
Async XLA Ops:
  0.6 0.7 %copy-start = (f32[30]{0:T(128)S(1)}, f32[30]{0:T(128)}, u32[]{:S(2)}) copy-start(f32[30]{0:T(128)} %wts.1) | copy-start | bytes 364

commit v2 on v1

--- a/solution.py
+++ b/solution.py
@@ -70,12 +70,12 @@
     return jnp.concatenate([x[-1:], x[:-1]], axis=0)
 
 
-def step_kernel(n_col, wts, u_h, v_h, t_h, s_h, eta_h, tu_h, tv_h, dep_h, cnt_h,
+def step_kernel(n_col, wts_h, u_h, v_h, t_h, s_h, eta_h, tu_h, tv_h, dep_h, cnt_h,
                 vu, vv, vt, vs, aux,
                 ub, vb, tb, sb, eta, ua, ubt, va, vbt, dep, cnt, cnt_i, fx, fy,
                 au, av, bu, bv, cu, cv, mu, mv, accu, accv, meanu, meanv,
-                pk, pkl, rx, rxl,
-                sem_in, sem_2d, sem_rs, sem_rr, sem_fs, sem_fr, sem_xs, sem_xr, sem_ls, sem_lr, sem_gs, sem_gr):
+                pk, pkl, rx, rxl, pkw, rxw, wts, sem_w, sem_half,
+                sem_in, sem_2d, sem_rs, sem_rr, sem_fs, sem_fr, sem_xs, sem_xr, sem_ls, sem_lr, sem_ws, sem_wr, sem_gs, sem_gr):
     col = lax.axis_index('col')
     row = lax.axis_index('row')
     east = lax.rem(col + 1, n_col)
@@ -91,7 +91,14 @@
     flats = ((eta_h, eta), (tu_h, ua), (tv_h, va), (dep_h, dep), (cnt_h, cnt_i))
 
     loads = {}
-    for c in (0, 3, 1, 2):
+    part = NR // 2
+    for c in range(1, NC - 1):
+        for f, (src, dst) in enumerate(cubes):
+            for h in range(2):
+                loads[f, c, h] = pltpu.make_async_copy(
+                    src.at[:, pl.ds(part * h, part), pl.ds(c * LN, LN)],
+                    dst.at[:, c, pl.ds(SL + part * h, part), :], sem_half.at[f, c - 1, h])
+    for c in (0, NC - 1):
         for f, (src, dst) in enumerate(cubes):
             loads[f, c] = pltpu.make_async_copy(
                 src.at[:, :, pl.ds(c * LN, LN)], dst.at[:, c, pl.ds(SL, NR), :], sem_in.at[f, c])
@@ -105,9 +112,8 @@
             loads[f, c].start()
     for copy in flat_loads:
         copy.start()
-    for c in (1, 2):
-        for f in range(4):
-            loads[f, c].start()
+    weight_load = pltpu.make_async_copy(wts_h, wts, sem_w)
+    weight_load.start()
 
     barrier = pltpu.get_barrier_semaphore()
     for peer in ({'col': east, 'row': row}, {'col': west, 'row': row}, {'col': col, 'row': other},
@@ -127,9 +133,7 @@
         for ref in (eta, ua, ubt, va, vbt, dep, cnt, fx, fy):
             ref[:, pl.ds(start, SL), :] = zero5
         cnt_i[:, pl.ds(start, SL), :] = jnp.zeros((NC, SL, LN), jnp.int32)
-        for d in range(2):
-            for p in range(2):
-                rx[d, p, pl.ds(start, SL), :] = jnp.zeros((SL, LN), jnp.float32)
+        rx[:, pl.ds(start, SL), :] = jnp.zeros((2, SL, LN), jnp.float32)
 
     pl.semaphore_wait(barrier, 5)
 
@@ -153,70 +157,78 @@
     for copy in row_copies + flat_copies:
         copy.start()
 
-    zero1 = jnp.zeros((SL, LN), jnp.float32)
+    groups = (NR // SL, SL, LN)
+    lanes = lax.broadcasted_iota(jnp.int32, (1, SL, LN), 2)
+    acc_e = acc_w = jnp.zeros(groups, jnp.float32)
     for f, (_, buf) in enumerate(cubes):
         loads[f, 0].wait()
-        loads[f, 3].wait()
-
-        @pl.loop(0, NR // 16)
-        def _(q):
-            for half_q in range(2):
-                r = 2 * q + half_q
-                rows = pl.ds(pl.multiple_of(SL + SL * r, SL), SL)
-                rows_o = pl.ds(pl.multiple_of(SL * r, SL), SL)
-                acc_e = zero1 if f == 0 else pk[0, 0, rows_o, :]
-                acc_w = zero1 if f == 0 else pk[1, 0, rows_o, :]
-                for k in range(LEVELS):
-                    m = f * LEVELS + k
-                    acc_e = jnp.where(lane == (m - 1) % LN, turn(buf[k, NC - 1, rows, :], m), acc_e)
-                    acc_w = jnp.where(lane == m, turn(buf[k, 0, rows, :], m), acc_w)
-                pk[0, 0, rows_o, :] = acc_e
-                pk[1, 0, rows_o, :] = acc_w
+        loads[f, NC - 1].wait()
+        for c in range(1, NC - 1):
+            loads[f, c, 0].start()
+        for k in range(LEVELS):
+            m = f * LEVELS + k
+            acc_e = jnp.where(lanes == (m - 1) % LN, turn(buf[k, NC - 1, pl.ds(SL, NR), :].reshape(groups), m), acc_e)
+            acc_w = jnp.where(lanes == m, turn(buf[k, 0, pl.ds(SL, NR), :].reshape(groups), m), acc_w)
+    for f in range(len(cubes)):
+        for c in range(1, NC - 1):
+            loads[f, c, 1].start()
 
     for copy in flat_loads:
         copy.wait()
-
-    @pl.loop(0, NR // SL)
-    def _(r):
-        rows_e = pl.ds(pl.multiple_of(own + SL * r, SL), SL)
-        rows_o = pl.ds(pl.multiple_of(SL * r, SL), SL)
-        acc_e = pk[0, 0, rows_o, :]
-        acc_w = pk[1, 0, rows_o, :]
-        for m, ref in ((LANE_COUNT, cnt_i), (LANE_DEPTH, dep)):
-            acc_e = jnp.where(lane == m - 1, turn(ref[NC - 1, rows_e, :].astype(jnp.float32), m), acc_e)
-            acc_w = jnp.where(lane == m, turn(ref[0, rows_e, :].astype(jnp.float32), m), acc_w)
-        pk[0, 0, rows_o, :] = acc_e
-        pk[1, 0, rows_o, :] = acc_w
-        acc_e = turn(eta[NC - 1, rows_e, :], HX)
-        acc_w = eta[0, rows_e, :]
-        for p, ref in ((1, ua), (2, va), (3, dep)):
-            here = lane >= p * HX
-            acc_e = jnp.where(here, turn(ref[NC - 1, rows_e, :], HX * (p + 1)), acc_e)
-            acc_w = jnp.where(here, turn(ref[0, rows_e, :], HX * p), acc_w)
-        pk[0, 1, rows_o, :] = acc_e
-        pk[1, 1, rows_o, :] = acc_w
+    for m, ref in ((LANE_COUNT, cnt_i), (LANE_DEPTH, dep)):
+        last = ref[NC - 1, pl.ds(own, NR), :].astype(jnp.float32).reshape(groups)
+        first = ref[0, pl.ds(own, NR), :].astype(jnp.float32).reshape(groups)
+        acc_e = jnp.where(lanes == m - 1, turn(last, m), acc_e)
+        acc_w = jnp.where(lanes == m, turn(first, m), acc_w)
+    pk[0] = acc_e.reshape(NR, LN)
+    pk[1] = acc_w.reshape(NR, LN)
+
+    def side_by_side(dst, refs):
+        for r in range(NR // SL):
+            rows_e = pl.ds(pl.multiple_of(own + SL * r, SL), SL)
+            acc_e = turn(refs[0][NC - 1, rows_e, :], HX)
+            acc_w = refs[0][0, rows_e, :]
+            for p, ref in enumerate(refs[1:], 1):
+                here = lane >= p * HX
+                acc_e = jnp.where(here, turn(ref[NC - 1, rows_e, :], HX * (p + 1)), acc_e)
+                acc_w = jnp.where(here, turn(ref[0, rows_e, :], HX * p), acc_w)
+            dst[0, pl.ds(SL * r, SL), :] = acc_e
+            dst[1, pl.ds(SL * r, SL), :] = acc_w
+
+    def sideways(src, dst, sends, recvs, from_row, to_row, rows):
+        copies = []
+        for d, side in enumerate((east, west)):
+            copies.append(pltpu.make_async_remote_copy(
+                src_ref=src.at[d], dst_ref=dst.at[d, pl.ds(own, NR), :],
+                send_sem=sends.at[d, 0], recv_sem=recvs.at[d, 0],
+                device_id={'col': side, 'row': row}, device_id_type=MESH))
+            copies.append(pltpu.make_async_remote_copy(
+                src_ref=src.at[d, pl.ds(from_row, rows), :], dst_ref=dst.at[d, pl.ds(to_row, rows), :],
+                send_sem=sends.at[d, 1], recv_sem=recvs.at[d, 1],
+                device_id={'col': side, 'row': other}, device_id_type=MESH))
+        return copies
+
+    corner = pl.multiple_of(PAD + HY - SL + (NR - HY + SL) * row, SL)
+    x_copies = sideways(pk, rx, sem_xs, sem_xr, edge_src, corner, SL)
+    for copy in x_copies:
+        copy.start()
+    side_by_side(pkw, (eta, ua, va, dep))
 
     for copy in flat_copies:
         copy.wait_recv()
     for r in range(STRIPS):
         cnt[0:NC, pl.ds(PAD + SL * r, SL), :] = cnt_i[:, pl.ds(PAD + SL * r, SL), :].astype(jnp.float32)
 
-    x_copies = []
-    for d, side in ((0, east), (1, west)):
-        x_copies.append(pltpu.make_async_remote_copy(
-            src_ref=pk.at[d], dst_ref=rx.at[d, :, pl.ds(own, NR), :],
-            send_sem=sem_xs.at[d, 0], recv_sem=sem_xr.at[d, 0],
-            device_id={'col': side, 'row': row}, device_id_type=MESH))
-        x_copies.append(pltpu.make_async_remote_copy(
-            src_ref=pk.at[d, :, pl.ds(near, HY), :], dst_ref=rx.at[d, :, pl.ds(far, HY), :],
-            send_sem=sem_xs.at[d, 1], recv_sem=sem_xr.at[d, 1],
-            device_id={'col': side, 'row': other}, device_id_type=MESH))
-    for copy in x_copies:
+
+    def inner_half(h):
+        for c in range(1, NC - 1):
+            for f in range(len(cubes)):
+                loads[f, c, h].wait()
+
+    inner_half(0)
+    w_copies = sideways(pkw, rxw, sem_ws, sem_wr, near, far, HY)
+    for copy in w_copies:
         copy.start()
-
-    for c in (1, 2):
-        for f in range(4):
-            loads[f, c].wait()
     for copy in row_copies:
         copy.wait_recv()
 
@@ -322,71 +334,67 @@
         def load(ref, k, dr=0):
             return ref[k, :, pl.ds(rb + dr, SL), :]
 
-        count, count_e, count_w = every(cnt[:, pl.ds(eb, SL), :])
-        lu = jnp.minimum(count, shift_e(count, count_e))
-        luw = jnp.minimum(count, shift_w(count, count_w))
+        count = cnt[:, pl.ds(eb, SL), :]
+        lu = jnp.minimum(count, ring_e(count))
+        count = count[:NC]
         lv = jnp.minimum(count, cnt[0:NC, pl.ds(eb + 1, SL), :])
         lvs = jnp.minimum(count, cnt[0:NC, pl.ds(eb - 1, SL), :])
-        half_dt = 0.5 * TIME_STEP
         carried = [None, None]
+        inside = count > 0.0
         for k in range(LEVELS):
             level = float(k)
-            u, _, uw = every(load(ub, k))
-            ge = jnp.where(lu > level, half_dt * u, 0.0)
-            gw = jnp.where(luw > level, half_dt * shift_w(u, uw), 0.0)
-            gn = jnp.where(lv > level, half_dt * load(vb, k)[:NC], 0.0)
-            gs = jnp.where(lvs > level, half_dt * load(vb, k, -1)[:NC], 0.0)
-            keep = 1.0 - (ge - gw + gn - gs)
-            inside = count > level
+            ge = TIME_STEP * jnp.where(lu > level, load(ub, k), 0.0)
+            ge, _, gw = every(ge)
+            gw = shift_w(ge, gw)
+            gn = TIME_STEP * jnp.where(lv > level, load(vb, k)[:NC], 0.0)
+            gs = TIME_STEP * jnp.where(lvs > level, load(vb, k, -1)[:NC], 0.0)
+            keep = 2.0 - (ge - gw + gn - gs)
+            inside_next = count > level + 1.0
+            ending = 0.5 * INV_D[k] * END_D[k]
+            pivot = ending if k == LEVELS - 1 else jnp.where(inside_next, 0.5 * INV_D[k], ending)
             for i, (buf, dst) in enumerate(((tb, vt), (sb, vs))):
                 q, qe, qw = every(load(buf, k))
-                new = keep * q - (ge * shift_e(q, qe) - gw * shift_w(q, qw)
-                                  + gn * load(buf, k, 1)[:NC] - gs * load(buf, k, -1)[:NC])
-                w = INV_D[k] * (new if k == 0 else new + DIFF_R * carried[i])
+                twice = keep * q - (ge * shift_e(q, qe) - gw * shift_w(q, qw)
+                                    + gn * load(buf, k, 1)[:NC] - gs * load(buf, k, -1)[:NC])
+                w = pivot * (twice if k == 0 else twice + 2.0 * DIFF_R * carried[i])
                 carried[i] = w
-                dst[k, :, out, :] = jnp.where(inside, w, new)
+                dst[k, :, out, :] = jnp.where(inside, w, q)
+            inside = inside_next
 
     @pl.loop(0, NR // SL)
     def _(r):
+        @pl.when(r == part // SL - 1)
+        def _():
+            inner_half(1)
+
         momentum(r, inner, (1, 2))
 
     for copy in x_copies:
         copy.wait_recv()
 
-    even = lax.rem(lane, 2) == 0
-
-    def unpack(r):
-        eb = pl.multiple_of(own + SL * r, SL)
-        from_west, from_east = rx[0, 0, pl.ds(eb, SL), :], rx[1, 0, pl.ds(eb, SL), :]
+    def unpack(rows, shape):
+        even = lax.rem(lanes if len(shape) == 3 else lane, 2) == 0
+        from_west, from_east = rx[0, rows, :].reshape(shape), rx[1, rows, :].reshape(shape)
         return jnp.where(even, from_east, from_west), jnp.where(even, from_west, from_east)
 
-    @pl.loop(0, NR // SL + 2)
-    def _(q):
-        r = q - 1
-        merged = unpack(r)
-        rows = pl.ds(pl.multiple_of(SL * q, SL), SL)
-        for f, (_, buf) in enumerate(cubes):
-            for k in range(LEVELS):
-                m = f * LEVELS + k
-                buf[k, NC, rows, :] = turn(merged[m % 2], -m)
-        rows = pl.ds(pl.multiple_of(own + SL * r, SL), SL)
-        cnt[NC, rows, :] = turn(merged[LANE_COUNT % 2], -LANE_COUNT)
-        dep[NC, rows, :] = turn(merged[LANE_DEPTH % 2], -LANE_DEPTH)
+    def unpack_cube(f, rows, merged):
+        for k in range(LEVELS):
+            m = f * LEVELS + k
+            cubes[f][1][k, NC, rows, :] = turn(merged[m % 2], -m).reshape(rows.size, LN)
+
+    merged = unpack(pl.ds(own, NR), groups)
+    for f in range(len(cubes)):
+        unpack_cube(f, pl.ds(SL, NR), merged)
+    cnt[NC, pl.ds(own, NR), :] = turn(merged[LANE_COUNT % 2], -LANE_COUNT).reshape(NR, LN)
+    dep[NC, pl.ds(own, NR), :] = turn(merged[LANE_DEPTH % 2], -LANE_DEPTH).reshape(NR, LN)
+    unpack_cube(1, pl.ds(0, SL), unpack(pl.ds(pl.multiple_of(own - SL, SL), SL), (SL, LN)))
+    unpack_cube(0, pl.ds(SL + NR, SL), unpack(pl.ds(pl.multiple_of(own + NR, SL), SL), (SL, LN)))
 
     @pl.loop(0, NR // SL)
     def _(r):
         momentum(r, outer, (0, 3))
 
-    for r in range(NR // SL):
-        rows_e = pl.ds(pl.multiple_of(own + SL * r, SL), SL)
-        acc_e = turn(fx[NC - 1, rows_e, :], HX)
-        acc_w = fx[0, rows_e, :]
-        for p, ref in ((1, fy), (2, cnt)):
-            here = lane >= p * HX
-            acc_e = jnp.where(here, turn(ref[NC - 1, rows_e, :], HX * (p + 1)), acc_e)
-            acc_w = jnp.where(here, turn(ref[0, rows_e, :], HX * p), acc_w)
-        pkl[0, pl.ds(SL * r, SL), :] = acc_e
-        pkl[1, pl.ds(SL * r, SL), :] = acc_w
+    side_by_side(pkl, (fx, fy, cnt))
 
     late = []
     for f, ref in enumerate((fx, fy)):
@@ -394,15 +402,7 @@
             src_ref=ref.at[pl.ds(0, NC), pl.ds(mid, HY), :], dst_ref=ref.at[pl.ds(0, NC), pl.ds(far, HY), :],
             send_sem=sem_gs.at[f], recv_sem=sem_gr.at[f],
             device_id={'col': col, 'row': other}, device_id_type=MESH))
-    for d, side in ((0, east), (1, west)):
-        late.append(pltpu.make_async_remote_copy(
-            src_ref=pkl.at[d], dst_ref=rxl.at[d, pl.ds(own, NR), :],
-            send_sem=sem_ls.at[d, 0], recv_sem=sem_lr.at[d, 0],
-            device_id={'col': side, 'row': row}, device_id_type=MESH))
-        late.append(pltpu.make_async_remote_copy(
-            src_ref=pkl.at[d, pl.ds(near, HY), :], dst_ref=rxl.at[d, pl.ds(far, HY), :],
-            send_sem=sem_ls.at[d, 1], recv_sem=sem_lr.at[d, 1],
-            device_id={'col': side, 'row': other}, device_id_type=MESH))
+    late += sideways(pkl, rxl, sem_ls, sem_lr, near, far, HY)
     for copy in late:
         copy.start()
 
@@ -410,16 +410,17 @@
     def _(r):
         tracers(r)
 
-    for copy in late:
+    for copy in w_copies + late:
         copy.wait_recv()
+    weight_load.wait()
 
     def strip(r, dr=0):
         return pl.ds(PAD + SL * r + dr, SL)
 
     for r in range(STRIPS):
         for p, ref, src in ((0, eta, 1), (1, ua, 1), (2, va, 1), (3, dep, 1), (0, fx, 2), (1, fy, 2), (2, cnt, 2)):
-            from_east = rx[1, 1, strip(r), :] if src == 1 else rxl[1, strip(r), :]
-            from_west = rx[0, 1, strip(r), :] if src == 1 else rxl[0, strip(r), :]
+            from_east = rxw[1, strip(r), :] if src == 1 else rxl[1, strip(r), :]
+            from_west = rxw[0, strip(r), :] if src == 1 else rxl[0, strip(r), :]
             ref[NC, strip(r), :] = jnp.where(
                 lane < HX, turn(from_east, -HX * p),
                 jnp.where(lane >= LN - HX, turn(from_west, LN - HX - HX * p), 0.0))
@@ -447,34 +448,52 @@
         accu[:, pl.ds(SL * r, SL), :] = jnp.zeros((NC, SL, LN), jnp.float32)
         accv[:, pl.ds(SL * r, SL), :] = jnp.zeros((NC, SL, LN), jnp.float32)
 
-    def subcycle(n, u_old, v_old, u_new, v_new, first):
+    def subcycle(n, u_old, v_old, u_new, v_new, span, first):
         weight = wts[n]
-        for r in range(STRIPS):
+        weight_old = wts[jnp.maximum(n - 1, 0)]
+        for r in span:
             rows = strip(r)
             u = u_old[:, rows, :]
             eta[:, rows, :] = eta[:, rows, :] - (u - ring_w(u) + v_old[:, rows, :] - v_old[:, strip(r, -1), :])
-        for r in range(STRIPS):
-            rows = strip(r)
+        for r in span:
+            rows, rows_a = strip(r), pl.ds(SL * r, SL)
             u, v, e = u_old[:, rows, :], v_old[:, rows, :], eta[:, rows, :]
             w2 = v + v_old[:, strip(r, -1), :]
             y2 = u + u_old[:, strip(r, 1), :]
-            if first:
-                u, v = mu[:, rows, :] * u, mv[:, rows, :] * v
-            u = u + (au[:, rows, :] * (w2 + ring_e(w2)) + bu[:, rows, :] - cu[:, rows, :] * (ring_e(e) - e))
-            v = v + (bv[:, rows, :] - av[:, rows, :] * (y2 + ring_w(y2)) - cv[:, rows, :] * (eta[:, strip(r, 1), :] - e))
-            u_new[:, rows, :] = u
-            v_new[:, rows, :] = v
-            rows_a = pl.ds(SL * r, SL)
-            accu[:, rows_a, :] = accu[:, rows_a, :] + weight * u[:NC]
-            accv[:, rows_a, :] = accv[:, rows_a, :] + weight * v[:NC]
-
-    subcycle(0, ua, va, ubt, vbt, True)
-    subcycle(1, ubt, vbt, ua, va, False)
-
-    @pl.loop(1, LEVELS // 2)
+            ug, vg = (mu[:, rows, :] * u, mv[:, rows, :] * v) if first else (u, v)
+            un = ug + (au[:, rows, :] * (w2 + ring_e(w2)) + bu[:, rows, :] - cu[:, rows, :] * (ring_e(e) - e))
+            vn = vg + (bv[:, rows, :] - av[:, rows, :] * (y2 + ring_w(y2))
+                       - cv[:, rows, :] * (eta[:, strip(r, 1), :] - e))
+            u_new[:, rows, :] = un
+            v_new[:, rows, :] = vn
+            if u_new is ua:
+                accu[:, rows_a, :] = accu[:, rows_a, :] + (weight_old * u[:NC] + weight * un[:NC])
+                accv[:, rows_a, :] = accv[:, rows_a, :] + (weight_old * v[:NC] + weight * vn[:NC])
+
+    def pair_of(pair, span, first):
+        subcycle(2 * pair, ua, va, ubt, vbt, span, first)
+        subcycle(2 * pair + 1, ubt, vbt, ua, va, span, False)
+
+    pair_of(0, range(STRIPS), True)
+
+    narrow = STRIPS - 2
+    turning = (SL * (STRIPS - narrow) - 2) // 2
+
+    @pl.loop(1, turning)
     def _(pair):
-        subcycle(2 * pair, ua, va, ubt, vbt, False)
-        subcycle(2 * pair + 1, ubt, vbt, ua, va, False)
+        pair_of(pair, range(STRIPS), False)
+
+    @pl.when(row == 0)
+    def _():
+        @pl.loop(turning, LEVELS // 2)
+        def _(pair):
+            pair_of(pair, range(narrow), False)
+
+    @pl.when(row == 1)
+    def _():
+        @pl.loop(turning, LEVELS // 2)
+        def _(pair):
+            pair_of(pair, range(STRIPS - narrow, STRIPS), False)
 
     @pl.loop(0, NR // SL)
     def _(r):
@@ -491,32 +510,61 @@
         aux[6, :, out, :] = (LEVELS / TIME_STEP) * ua[0:NC, rows, :]
         aux[7, :, out, :] = (LEVELS / TIME_STEP) * va[0:NC, rows, :]
 
-    for copy in row_copies + flat_copies + x_copies + late:
+    for copy in row_copies + flat_copies + x_copies + w_copies + late:
         copy.wait_send()
 
 
-def finish_kernel(vu, vv, vt, vs, aux, o_eta, o_tu, o_tv, o_u, o_v, o_t, o_s):
-    for c in range(NC):
-        cols = pl.ds(c * LN, LN)
-        o_eta[:, cols] = aux[5, c]
-        o_tu[:, cols] = aux[6, c]
-        o_tv[:, cols] = aux[7, c]
-        count, lu, lv = aux[0, c], aux[1, c], aux[2, c]
-        gu, gv = aux[3, c], aux[4, c]
-        xu = xv = xt = xs = jnp.zeros((SL, LN), jnp.float32)
-        for k in reversed(range(LEVELS)):
-            level = float(k)
-            last = count == level + 1.0
-            inside = count > level
-            wu, wv, wt, ws = vu[k, c], vv[k, c], vt[k, c], vs[k, c]
-            xu = jnp.where(lu == level + 1.0, END_V[k] * wu, wu + CARRY_V[k] * xu)
-            xv = jnp.where(lv == level + 1.0, END_V[k] * wv, wv + CARRY_V[k] * xv)
-            xt = jnp.where(last, END_D[k] * wt, wt + CARRY_D[k] * xt)
-            xs = jnp.where(last, END_D[k] * ws, ws + CARRY_D[k] * xs)
-            o_u[k, :, cols] = jnp.where(lu > level, xu + gu, 0.0)
-            o_v[k, :, cols] = jnp.where(lv > level, xv + gv, 0.0)
-            o_t[k, :, cols] = jnp.where(inside, xt, wt)
-            o_s[k, :, cols] = jnp.where(inside, xs, ws)
+def finish_kernel(vu, vv, vt, vs, aux, o_eta, o_tu, o_tv, o_u, o_v, o_t, o_s, *scratch):
+    flat_bufs, cube_bufs, sem_f, sem_c = scratch[:3], scratch[3:7], scratch[7], scratch[8]
+    flat_copies = []
+    for i, (buf, ref) in enumerate(zip(flat_bufs, (o_eta, o_tu, o_tv))):
+        for c in range(NC):
+            buf[:, pl.ds(c * LN, LN)] = aux[5 + i, c]
+        flat_copies.append(pltpu.make_async_copy(buf, ref, sem_f.at[i]))
+
+    def copies(r):
+        rows = pl.ds(SL * r if isinstance(r, int) else pl.multiple_of(SL * r, SL), SL)
+        return [pltpu.make_async_copy(buf.at[:, rows, :], ref.at[:, rows, :], sem_c.at[i, r])
+                for i, (buf, ref) in enumerate(zip(cube_bufs, (o_u, o_v, o_t, o_s)))]
+
+    @pl.loop(0, NR // SL)
+    def _(r):
+        finish_rows(pl.ds(pl.multiple_of(SL * r, SL), SL), vu, vv, vt, vs, aux, *cube_bufs)
+        for copy in copies(r):
+            copy.start()
+
+    for copy in flat_copies:
+        copy.start()
+    for r in range(NR // SL):
+        for copy in copies(r):
+            copy.wait()
+    for copy in flat_copies:
+        copy.wait()
+
+
+def finish_rows(rows, vu, vv, vt, vs, aux, o_u, o_v, o_t, o_s):
+    def put(ref, value):
+        for c in range(NC):
+            ref[rows, pl.ds(c * LN, LN)] = value[c]
+
+    count, lu, lv, gu, gv = (aux[i, :, rows, :] for i in range(5))
+    xu = xv = xt = xs = on_u = on_v = inside = None
+    for k in reversed(range(LEVELS)):
+        level = float(k)
+        wu, wv, xt_new, xs_new = (ref[k, :, rows, :] for ref in (vu, vv, vt, vs))
+        if k == LEVELS - 1:
+            xu, xv = END_V[k] * wu, END_V[k] * wv
+        else:
+            xu = jnp.where(on_u, wu + CARRY_V[k] * xu, END_V[k] * wu)
+            xv = jnp.where(on_v, wv + CARRY_V[k] * xv, END_V[k] * wv)
+            xt_new = xt_new + CARRY_D[k] * jnp.where(inside, xt, 0.0)
+            xs_new = xs_new + CARRY_D[k] * jnp.where(inside, xs, 0.0)
+        xt, xs = xt_new, xs_new
+        on_u, on_v, inside = lu > level, lv > level, count > level
+        put(o_u.at[k], jnp.where(on_u, xu + gu, 0.0))
+        put(o_v.at[k], jnp.where(on_v, xv + gv, 0.0))
+        put(o_t.at[k], xt)
+        put(o_s.at[k], xs)
 
 
 def solution(mesh):
@@ -535,30 +583,28 @@
         swept_all = pl.pallas_call(
             functools.partial(step_kernel, n_col),
             out_shape=(swept,) * 4 + (jax.ShapeDtypeStruct((SL, NC, NR, LN), f32),),
-            in_specs=[pl.BlockSpec(memory_space=pltpu.SMEM)] + [anywhere] * 9,
+            in_specs=[anywhere] * 10,
             out_specs=(vmem,) * 5,
             scratch_shapes=[cube] * 4 + [wide] * 7 + [pltpu.VMEM((NC, EROWS, LN), jnp.int32)] + [wide] * 10
             + [acc, acc, mean, mean,
-               pltpu.VMEM((2, 2, NR, LN), f32), pltpu.VMEM((2, NR, LN), f32),
-               pltpu.VMEM((2, 2, EROWS, LN), f32), pltpu.VMEM((2, EROWS, LN), f32)]
+               *[pltpu.VMEM((2, rows, LN), f32) for rows in (NR, NR, EROWS, EROWS, NR, EROWS)],
+               pltpu.SMEM((LEVELS,), f32), dma(()), dma((4, NC - 2, 2))]
             + [dma((4, NC)), dma((5, NC)), dma((4, NC)), dma((4, NC)), dma((5, NC)), dma((5, NC)),
-               dma((2, 2)), dma((2, 2)), dma((2, 2)), dma((2, 2)), dma((2,)), dma((2,))],
+               *[dma((2, 2))] * 6, dma((2,)), dma((2,))],
             compiler_params=pltpu.CompilerParams(
                 collective_id=0, has_side_effects=True, vmem_limit_bytes=33 * 1024 * 1024),
             name='step_kernel',
-        )(avg_weights, *[pltpu.with_memory_space_constraint(x, pltpu.HBM) for x in (vel_u, vel_v, temperature, salinity, surf_eta, trans_u, trans_v, bottom_depth, level_count)])
+        )(*[pltpu.with_memory_space_constraint(x, pltpu.HBM) for x in (avg_weights, vel_u, vel_v, temperature, salinity, surf_eta, trans_u, trans_v, bottom_depth, level_count)])
         flat_out = jax.ShapeDtypeStruct(surf_eta.shape, f32)
         cube_out = jax.ShapeDtypeStruct(vel_u.shape, f32)
-        flat_spec = pl.BlockSpec((SL, NC * LN), lambda r: (r, 0))
-        cube_spec = pl.BlockSpec((LEVELS, SL, NC * LN), lambda r: (0, r, 0))
-        in_spec = pl.BlockSpec((LEVELS, NC, SL, LN), lambda r: (0, 0, r, 0))
         return pl.pallas_call(
             finish_kernel,
-            grid=(NR // SL,),
             out_shape=(flat_out,) * 3 + (cube_out,) * 4,
-            in_specs=[in_spec] * 4 + [pl.BlockSpec((SL, NC, SL, LN), lambda r: (0, 0, r, 0))],
-            out_specs=(flat_spec,) * 3 + (cube_spec,) * 4,
-            compiler_params=pltpu.CompilerParams(vmem_limit_bytes=16 * 1024 * 1024),
+            in_specs=[vmem] * 5,
+            out_specs=(anywhere,) * 7,
+            scratch_shapes=[pltpu.VMEM(surf_eta.shape, f32)] * 3 + [pltpu.VMEM(vel_u.shape, f32)] * 4
+            + [dma((3,)), dma((4, NR // SL))],
+            compiler_params=pltpu.CompilerParams(vmem_limit_bytes=20 * 1024 * 1024),
             name='finish_kernel',
         )(*swept_all)
 

time: 51.9 us -> 46 us (0.89)
  Pallas kernels: 50.5 us -> 45.2 us
  local copies, waits for them, and re-layouts: 0.65 us -> 0 us
    pallas_call x1, Pallas kernels: 8.73 us -> 6.04 us  [step(): pl.pallas_call(finish_kernel, out_shape=(flat_out,) * 3 + (cube_out,) * 4...]
    pallas_call x1, Pallas kernels: 41.7 us -> 39.2 us  [step(): pl.pallas_call(functools.partial(step_kernel, n_col), out_shape=(swept,)...]
    unnamed x2 -> x0, local copies, waits for them, and re-layouts: 0.65 us -> none
where the time goes in v2:
time: 46 us; the launch traced here: 45.9 us
  Pallas kernels  45.2 us (98%)
  between operations  0.64 us (1%)
    pallas_call x1, Pallas kernels, step(): pl.pallas_call(functools.partial(step_kernel, n_col), out_shape=(swept,)...  39.2 us
    pallas_call x1, Pallas kernels, step(): pl.pallas_call(finish_kernel, out_shape=(flat_out,) * 3 + (cube_out,) * 4...  6.04 us

profile of v2, /device:TPU:0, one launch (start us, length us, event | category | flops | bytes accessed | tf_op | source)
XLA Modules:
  0.0 45.9 jit_solution(6015036257686915409)
XLA Ops:
  0.6 39.2 %step_kernel.1 = (f32[30,4,64,128]{3,2,1,0:T(8,128)S(1)}, f32[30,4,64,128]{3,2,1,0:T(8,128)S(1)}, f32[30,4,64,128]{3,2,1,0:T(8,128)S(1)}, f32[30,4,64,128]{3,2,1,0:T(8,128)S(1)}, f32[8,4,64,128]{3,2,1,0:T(8,128)S(1)}) custom-call(f32[30]{0:T(128)} %wts_h.1, f32[30,64,512]{2,1,0:T(8,128)} %u_h.1, f32[30,64,512]{2,1,0:T(8,128)} %v_h.1, f32[30,64,512]{2,1,0:T(8,128)} %t_h.1, ...), custom_call_target="tpu_custom_call" | custom-call | tf_op jit(solution)/shard_map/step_kernel/pallas_call | solution.py:583
  39.8 6.0 %finish_kernel.1 = (f32[64,512]{1,0:T(8,128)}, f32[64,512]{1,0:T(8,128)}, f32[64,512]{1,0:T(8,128)}, f32[30,64,512]{2,1,0:T(8,128)}, f32[30,64,512]{2,1,0:T(8,12...) custom-call(f32[30,4,64,128]{3,2,1,0:T(8,128)S(1)} %get-tuple-element.12.vu, ...), custom_call_target="tpu_custom_call" | custom-call | tf_op jit(solution)/shard_map/finish_kernel/pallas_call | solution.py:600
